TPU v7x, 32 devices: a whole 2x2x4 slice. The times are simulated.
32 devices in a mesh: row: 4 (over y, x), col: 4 (over z), crop: 2 (over core).
Axes of the slice: x: 2, y: 2, z: 4, core: 2. Of those that a mesh axis runs over, the one named last changes fastest.
Arguments:
- pair_repr: bfloat16 [256, 128, 128], P(('crop', 'row'), 'col'), parts along dimension 0, may hold values from -6 to 6
- pair_mask: int32 [256, 128], P(('crop', 'row'), 'col'), parts along dimension 0, may hold values 0 or 1
- out_left_w: bfloat16 [128, 256], replicated, may hold values from -0.5 to 0.5
- out_right_w: bfloat16 [128, 256], replicated, may hold values from -0.5 to 0.5
- out_gate_w: bfloat16 [128, 128], replicated, may hold values from -0.5 to 0.5
- out_final_w: bfloat16 [128, 128], replicated, may hold values from -0.5 to 0.5
- in_left_w: bfloat16 [128, 256], replicated, may hold values from -0.5 to 0.5
- in_right_w: bfloat16 [128, 256], replicated, may hold values from -0.5 to 0.5
- in_gate_w: bfloat16 [128, 128], replicated, may hold values from -0.5 to 0.5
- in_final_w: bfloat16 [128, 128], replicated, may hold values from -0.5 to 0.5
- trans_in_w: bfloat16 [128, 1024], replicated, may hold values from -0.5 to 0.5
- trans_out_w: bfloat16 [512, 128], replicated, may hold values from -0.25 to 0.25
Outputs:
- pair_out: bfloat16 [256, 128, 128], P(('crop', 'row'), 'col'), parts along dimension 0
There are 2 independent parts, one for each index of `crop`. A program takes and returns all parts, laid end to end along the dimension named above; an argument that names none is the same for every part. Nothing has to cross between parts.
All inputs are finite; a program needn't handle non-finite values. No bound on the sum of `pair_mask` on one device may be relied on, other than what follows from the above.
Results may differ from a plain program's by a relative error of at most 0.015.
Values may be sent and summed in bfloat16 or wider, within the bound.
No kernel may reach another device: no remote copies, remote signals or barrier semaphores. Data moves between devices by JAX's collectives and lax.ppermute only.
A program may use at most 128 MiB of HBM per device.

v0:
```python
import jax
import jax.numpy as jnp
from jax import lax
from jax.sharding import PartitionSpec as P

epsilon = 1e-05


def layer_norm(values):
    average = jnp.mean(values, axis=-1, keepdims=True)
    centered = values - average
    spread = jnp.mean(centered * centered, axis=-1, keepdims=True)
    return centered * lax.rsqrt(spread + epsilon)


def gated(normed, weight, mask_vals):
    projected = jnp.dot(normed, weight, preferred_element_type=jnp.float32)
    half_width = weight.shape[1] // 2
    result = jax.nn.sigmoid(projected[..., :half_width]) * projected[..., half_width:]
    result = result * mask_vals[..., None]
    return result.astype(jnp.bfloat16)


def finish(pair_repr, normed, triangle, gate_w, final_w):
    gate_vals = jax.nn.sigmoid(jnp.dot(normed, gate_w, preferred_element_type=jnp.float32))
    tri_norm = layer_norm(triangle).astype(jnp.bfloat16)
    update = jnp.dot(tri_norm, final_w, preferred_element_type=jnp.float32)
    return (pair_repr.astype(jnp.float32) + gate_vals * update).astype(jnp.bfloat16)


def shards(
    pair_repr,
    pair_mask,
    out_left_w,
    out_right_w,
    out_gate_w,
    out_final_w,
    in_left_w,
    in_right_w,
    in_gate_w,
    in_final_w,
    trans_in_w,
    trans_out_w,
):
    mask_vals = pair_mask.astype(jnp.float32)
    normed_out = layer_norm(pair_repr.astype(jnp.float32)).astype(jnp.bfloat16)
    outbound = gated(normed_out, out_right_w, mask_vals)
    turned_right = lax.all_to_all(
        lax.all_to_all(outbound, "row", split_axis=0, concat_axis=0, tiled=True),
        "col",
        split_axis=0,
        concat_axis=1,
        tiled=True,
    )
    left_tile = gated(normed_out, out_left_w, mask_vals)
    gathered = lax.all_gather(left_tile, "col", axis=1, tiled=True)
    triangle = jnp.einsum(
        "ikh,jkh->ijh",
        gathered,
        lax.all_gather(turned_right, "row", axis=0, tiled=True),
        preferred_element_type=jnp.float32,
    )
    middle = finish(pair_repr, normed_out, triangle, out_gate_w, out_final_w)
    normed_in = layer_norm(middle.astype(jnp.float32)).astype(jnp.bfloat16)
    outbound_left = gated(normed_in, in_left_w, mask_vals)
    turned_left = lax.all_to_all(
        lax.all_to_all(outbound_left, "col", split_axis=1, concat_axis=1, tiled=True),
        "row",
        split_axis=1,
        concat_axis=0,
        tiled=True,
    )
    right_tile = gated(normed_in, in_right_w, mask_vals)
    column_panel = lax.all_gather(right_tile, "row", axis=0, tiled=True)
    triangle_in = jnp.einsum(
        "kih,kjh->ijh",
        lax.all_gather(turned_left, "col", axis=1, tiled=True),
        column_panel,
        preferred_element_type=jnp.float32,
    )
    after_in = finish(middle, normed_in, triangle_in, in_gate_w, in_final_w)
    normed_mix = layer_norm(after_in.astype(jnp.float32)).astype(jnp.bfloat16)
    projected = jnp.dot(normed_mix, trans_in_w, preferred_element_type=jnp.float32)
    half_width = trans_in_w.shape[1] // 2
    hidden = (jax.nn.silu(projected[..., :half_width]) * projected[..., half_width:]).astype(
        jnp.bfloat16
    )
    result = after_in.astype(jnp.float32) + jnp.dot(
        hidden, trans_out_w, preferred_element_type=jnp.float32
    )
    return result.astype(jnp.bfloat16)


def solution(mesh):
    in_specs = (
        P(("crop", "row"), "col", None),
        P(("crop", "row"), "col"),
        P(),
        P(),
        P(),
        P(),
        P(),
        P(),
        P(),
        P(),
        P(),
        P(),
    )
    out_specs = P(("crop", "row"), "col", None)
    return jax.shard_map(shards, mesh=mesh, in_specs=in_specs, out_specs=out_specs, check_vma=False)
```

profile of v0, /device:TPU:0, one launch (start us, length us, event | category | flops | bytes accessed | tf_op | source)
XLA Modules:
  0.0 162.0 jit_solution(13725264176336256992)
XLA Ops:
  6.5 0.0 copy-start
  6.5 0.0 all-gather.7.cloned.1.call-start
  6.5 1.2 convert_reduce_fusion
  7.8 1.3 fusion.17
  9.1 1.4 fusion.44
  10.5 0.0 copy-done.1
  10.6 1.3 fusion.46
  11.9 0.0 copy-done.6
  11.9 0.0 copy-start.8
  11.9 1.0 fusion.30
  12.9 0.0 all-gather.7.cloned.1.call-update
  12.9 0.0 all-gather.5.cloned.1.call-start
  13.0 10.7 %all_to_all.46 = bf16[32,32,128]{2,1,0:T(8,128)(2,1)S(1)} all-to-all(bf16[32,32,128]{2,1,0:T(8,128)(2,1)S(1)} %get-tuple-element.8), channel_id=1, replica_groups=mesh['row'=4,'col'=4,'crop'=2] {'row'}, dimensions={0} | all-to-all | bytes 524288 | tf_op jit(solution)/shard_map/all_to_all | solution.py:49
  23.7 21.0 %all_to_all.47 = bf16[32,32,128]{2,1,0:T(8,128)(2,1)S(1)} all-to-all(bf16[32,32,128]{2,1,0:T(8,128)(2,1)S(1)} %all_to_all.46), channel_id=1, replica_groups=mesh['row'=4,'col'=4,'crop'=2] {'col'}, dimensions={0} | all-to-all | bytes 524288 | tf_op jit(solution)/shard_map/all_to_all | solution.py:48
  44.7 0.9 copy.66
  45.6 0.0 all-gather.5.cloned.1.call-update
  45.7 0.0 all-gather.9.cloned.1.call-start
  45.7 0.0 copy-done.8
  45.7 0.7 fusion.6
  46.5 3.4 %all-gather.7.cloned.1.call-done = bf16[32,128,128]{2,1,0:T(8,128)(2,1)} async-done(((bf16[32,32,128]{2,1,0:T(8,128)(2,1)}), bf16[32,128,128]{2,1,0:T(8,128)(2,1)}) %all-gather.7.cloned.1.call-update) | async-done | bytes 1048592 | tf_op jit(solution)/shard_map/all_gather | solution.py:56
  49.9 2.7 %copy.67 = bf16[32,128,128]{1,0,2:T(8,128)(2,1)} copy(bf16[32,128,128]{2,1,0:T(8,128)(2,1)} %all-gather.7.cloned.1.call-done) | data formatting | bytes 2097152 | tf_op jit(solution)/shard_map/all_gather | solution.py:56
  52.5 24.4 %all-gather.5.cloned.1.call-done = bf16[32,128,128]{1,0,2:T(8,128)(2,1)} async-done(((bf16[8,128,128]{1,0,2:T(8,128)(2,1)}), bf16[32,128,128]{1,0,2:T(8,128)(2,1)}) %all-gather.5.cloned.1.call-update) | async-done | bytes 1048592 | tf_op jit(solution)/shard_map/all_gather | solution.py:60
  76.9 2.2 %bitcast_reduce_fusion.1 = (f32[32,32]{0,1:T(8,128)S(1)}, f32[128,32,32]{2,1,0:T(8,128)S(1)}) fusion(bf16[32,128,128]{1,0,2:T(8,128)(2,1)} %all-gather.5.cloned.1.call-done, bf16[32,128,128]{1,0,2:T(8,128)(2,1)} %copy.67), kind=kOutput, calls=%fused_computation.5 | convolution fusion | flops 33684480 | bytes 2625536 | tf_op jit(solution)/shard_map/ikh,jkh->ijh/dot_general | solution.py:57
  79.2 0.1 copy.68
  79.2 0.1 copy.69
  79.3 0.3 multiply_reduce_fusion.1
  79.6 0.1 copy.70
  79.7 0.1 copy.71
  79.8 1.3 multiply_convert_fusion.1
  81.1 2.7 %copy.72 = bf16[32,32,128]{2,1,0:T(8,128)(2,1)S(1)} copy(bf16[32,32,128]{0,1,2:T(8,128)(2,1)} %multiply_convert_fusion.1) | data formatting | bytes 524288 | tf_op jit(solution)/shard_map/convert_element_type | solution.py:26
  83.7 0.0 copy-done.5
  83.7 0.0 copy-start.3
  83.8 0.4 fusion.60
  84.1 0.4 multiply_reduce_fusion.3
  84.5 0.3 multiply_convert_fusion.3
  84.9 0.3 fusion.49
  85.2 0.3 fusion.51
  85.5 1.0 fusion.20
  86.5 0.0 all-gather.9.cloned.1.call-update
  86.5 0.0 all-gather.11.cloned.1.call-start
  86.5 0.1 copy.73
  86.7 13.1 %all_to_all.48 = bf16[32,32,128]{2,0,1:T(8,128)(2,1)S(1)} all-to-all(bf16[32,32,128]{2,0,1:T(8,128)(2,1)S(1)} %copy.73), channel_id=1, replica_groups=mesh['row'=4,'col'=4,'crop'=2] {'col'}, dimensions={1} | all-to-all | bytes 524288 | tf_op jit(solution)/shard_map/all_to_all | solution.py:67
  99.8 8.2 %all_to_all.49 = bf16[32,32,128]{2,0,1:T(8,128)(2,1)S(1)} all-to-all(bf16[32,32,128]{2,0,1:T(8,128)(2,1)S(1)} %all_to_all.48), channel_id=1, replica_groups=mesh['row'=4,'col'=4,'crop'=2] {'row'}, dimensions={1} | all-to-all | bytes 524288 | tf_op jit(solution)/shard_map/all_to_all | solution.py:66
  108.0 0.1 copy.75
  108.1 0.9 copy.76
  109.0 0.0 all-gather.11.cloned.1.call-update
  109.1 1.1 fusion.3
  110.2 3.4 %all-gather.9.cloned.1.call-done = bf16[128,32,128]{2,1,0:T(8,128)(2,1)} async-done(((bf16[32,32,128]{2,1,0:T(8,128)(2,1)}), bf16[128,32,128]{2,1,0:T(8,128)(2,1)}) %all-gather.9.cloned.1.call-update) | async-done | bytes 1048592 | tf_op jit(solution)/shard_map/all_gather | solution.py:74
  113.6 3.2 %copy.77 = bf16[128,32,128]{0,1,2:T(8,128)(2,1)} copy(bf16[128,32,128]{2,1,0:T(8,128)(2,1)} %all-gather.9.cloned.1.call-done) | data formatting | bytes 2097152 | tf_op jit(solution)/shard_map/all_gather | solution.py:74
  116.8 27.7 %all-gather.11.cloned.1.call-done = bf16[128,32,128]{0,1,2:T(8,128)(2,1)} async-done(((bf16[128,8,128]{0,1,2:T(8,128)(2,1)}), bf16[128,32,128]{0,1,2:T(8,128)(2,1)}) %all-gather.11.cloned.1.call-update) | async-done | bytes 1048592 | tf_op jit(solution)/shard_map/all_gather | solution.py:77
  144.5 2.2 %bitcast_reduce_fusion = (f32[32,32]{0,1:T(8,128)S(1)}, f32[128,32,32]{2,1,0:T(8,128)S(1)}) fusion(bf16[128,32,128]{0,1,2:T(8,128)(2,1)} %copy.77, bf16[128,32,128]{0,1,2:T(8,128)(2,1)} %all-gather.11.cloned.1.call-done), kind=kOutput, calls=%fused_computation.3 | convolution fusion | flops 33684480 | bytes 2625536 | tf_op jit(solution)/shard_map/kih,kjh->ijh/dot_general | solution.py:75
  146.7 0.1 copy.78
  146.8 0.1 copy.79
  146.9 0.3 multiply_reduce_fusion
  147.2 0.1 copy.80
  147.3 0.1 copy.81
  147.4 1.3 multiply_convert_fusion
  148.6 2.6 %copy.82 = bf16[32,32,128]{2,1,0:T(8,128)(2,1)S(1)} copy(bf16[32,32,128]{0,1,2:T(8,128)(2,1)} %multiply_convert_fusion) | data formatting | bytes 524288 | tf_op jit(solution)/shard_map/convert_element_type | solution.py:26
  151.3 1.4 fusion.61
  152.7 0.4 multiply_reduce_fusion.2
  153.1 0.0 copy-start.7
  153.1 0.8 fusion.39
  153.9 0.1 copy-done.7
  154.0 1.4 fusion.13
  (23 shorter events, 0.1 us)
Async XLA Ops:
  6.5 146.6 %copy-start = (bf16[128,1024]{1,0:T(8,128)(2,1)S(1)}, bf16[128,1024]{1,0:T(8,128)(2,1)}, u32[]{:S(2)}) copy-start(bf16[128,1024]{1,0:T(8,128)(2,1)} %param.22) | copy-start | bytes 786436
  6.5 4.0 %copy-start.1 = (bf16[32,32,128]{2,1,0:T(8,128)(2,1)S(1)}, bf16[32,32,128]{2,1,0:T(8,128)(2,1)}, u32[]{:S(2)}) copy-start(bf16[32,32,128]{2,1,0:T(8,128)(2,1)} %param.12) | copy-start | bytes 786436
  6.5 5.3 %copy-start.6 = (s32[32,32]{1,0:T(8,128)S(1)}, s32[32,32]{1,0:T(8,128)}, u32[]{:S(2)}) copy-start(s32[32,32]{1,0:T(8,128)} %param.13) | copy-start | bytes 12292
  6.5 43.3 %all-gather.7.cloned.1.call-start = ((), (), s32[]{:S(2)}) async-start(), calls=%async_computation.5 | async-start | bytes 1310720 | tf_op jit(solution)/shard_map/all_gather | solution.py:56
  11.9 33.8 %copy-start.8 = (bf16[128,128]{1,0:T(8,128)(2,1)S(1)}, bf16[128,128]{1,0:T(8,128)(2,1)}, u32[]{:S(2)}) copy-start(bf16[128,128]{1,0:T(8,128)(2,1)} %param.16) | copy-start | bytes 98308
  12.9 64.0 %all-gather.5.cloned.1.call-start = ((), (), s32[]{:S(2)}) async-start(), calls=%async_computation.4 | async-start | bytes 1310720 | tf_op jit(solution)/shard_map/all_gather | solution.py:60
  45.7 67.9 %all-gather.9.cloned.1.call-start = ((), (), s32[]{:S(2)}) async-start(), calls=%async_computation.6 | async-start | bytes 1310720 | tf_op jit(solution)/shard_map/all_gather | solution.py:74
  79.8 3.9 %copy-start.5 = (bf16[128,128]{1,0:T(8,128)(2,1)S(1)}, bf16[128,128]{1,0:T(8,128)(2,1)}, u32[]{:S(2)}) copy-start(bf16[128,128]{1,0:T(8,128)(2,1)} %param.17) | copy-start | bytes 98308
  81.1 3.8 %copy-start.2 = (bf16[128,256]{1,0:T(8,128)(2,1)S(1)}, bf16[128,256]{1,0:T(8,128)(2,1)}, u32[]{:S(2)}) copy-start(bf16[128,256]{1,0:T(8,128)(2,1)} %param.18) | copy-start | bytes 196612
  83.7 1.4 copy-start.3
  86.5 22.6 %copy-start.9 = (bf16[128,128]{1,0:T(8,128)(2,1)S(1)}, bf16[128,128]{1,0:T(8,128)(2,1)}, u32[]{:S(2)}) copy-start(bf16[128,128]{1,0:T(8,128)(2,1)} %param.20) | copy-start | bytes 98308
  86.5 58.0 %all-gather.11.cloned.1.call-start = ((), (), s32[]{:S(2)}) async-start(), calls=%async_computation.7 | async-start | bytes 1310720 | tf_op jit(solution)/shard_map/all_gather | solution.py:77
  147.4 3.9 %copy-start.4 = (bf16[128,128]{1,0:T(8,128)(2,1)S(1)}, bf16[128,128]{1,0:T(8,128)(2,1)}, u32[]{:S(2)}) copy-start(bf16[128,128]{1,0:T(8,128)(2,1)} %param.21) | copy-start | bytes 98308
  153.1 0.9 copy-start.7
Sparse Core Ops, SparseCore 0:
  13.1 36.7 all-gather.6
  51.7 25.2 all-gather.4
  86.6 26.9 all-gather.8
  115.0 29.4 all-gather.10
where the time goes:
time: 163 us; the launch traced here: 162 us
  waiting for transfers between devices  59 us (36%)
  blocking collectives  53.1 us (33%)
  local copies, waits for them, and re-layouts  14 us (9%)
  matrix products  13.4 us (8%)
  between operations  13.4 us (8%)
  other arithmetic  8.94 us (5%)
    all_gather x1, waiting for transfers between devices, shards(): lax.all_gather(turned_left, 'col', axis=1, tiled=True)  27.7 us
    all_gather x1, waiting for transfers between devices, shards(): lax.all_gather(turned_right, 'row', axis=0, tiled=True)  24.4 us
    all_to_all x1, blocking collectives, shards(): lax.all_to_all(lax.all_to_all(outbound, 'row', split_axis=0, concat_axis=...  21 us
    all_to_all x1, blocking collectives, shards(): lax.all_to_all(outbound_left, 'col', split_axis=1, concat_axis=1, tiled=T...  13.1 us
    all_to_all x1, blocking collectives, shards(): lax.all_to_all(outbound, 'row', split_axis=0, concat_axis=0, tiled=True)  10.7 us
    all_to_all x1, blocking collectives, shards(): lax.all_to_all(lax.all_to_all(outbound_left, 'col', split_axis=1, concat_...  8.25 us
    convert_element_type x2, local copies, waits for them, and re-layouts, finish(): tri_norm = layer_norm(triangle).astype(jnp.bfloat16)  5.27 us
    all_gather x1, waiting for transfers between devices, shards(): column_panel = lax.all_gather(right_tile, 'row', axis=0, tiled=True)  3.41 us
  transfers between devices with their start and end apart: 4, of which 4 were waited for; matrix products, arithmetic and copies ran while one was open for 6% of the time, Pallas kernels for 0%

commit v1 on v0

v1 whole, which is shorter than its diff:
```python
import functools

import jax
import jax.numpy as jnp
from jax import lax
from jax.experimental import pallas as pl
from jax.experimental.pallas import tpu as pltpu
from jax.sharding import PartitionSpec as P

epsilon = 1e-05
LANES = 128
SUB = 8
F32, BF16 = jnp.float32, jnp.bfloat16


def norm_rows(values):
    average = jnp.mean(values, axis=0, keepdims=True)
    centered = values - average
    spread = jnp.mean(centered * centered, axis=0, keepdims=True)
    return (centered * lax.rsqrt(spread + epsilon)).astype(BF16)


def sigmoid(values):
    return 0.5 * jnp.tanh(0.5 * values) + 0.5


def dot(a, b):
    return jnp.dot(a, b, preferred_element_type=F32)


def swap_groups(values, width):
    values = list(values)
    count = len(values)
    group = lax.broadcasted_iota(jnp.int32, values[0].shape, 1) // width
    bit = count // 2
    while bit:
        low = (group & bit) == 0
        for at in range(count):
            if at & bit:
                continue
            one, two = values[at], values[at | bit]
            values[at] = jnp.where(low, one, pltpu.roll(two, bit * width, 1))
            values[at | bit] = jnp.where(low, pltpu.roll(one, LANES - bit * width, 1), two)
        bit //= 2
    return values


def lane_mask(mask_ref, lane_ref, groups):
    rows, width = mask_ref.shape
    count = rows // groups
    for lo in range(groups):
        lane_ref[:, lo * width : (lo + 1) * width] = mask_ref[lo * count : (lo + 1) * count, :].astype(F32)


def project(normed, step, per, left_w, right_w, gate_w, lane_ref, scr_ref, gate_ref):
    half = left_w.shape[0] // 2
    high = lane_ref.shape[0]
    for side, weight in enumerate((left_w, right_w)):
        both = dot(weight, normed)
        value = sigmoid(both[:half]) * both[half:]
        for u in range(per):
            hi = step * per + u
            piece = value[:, u * LANES : (u + 1) * LANES] * lane_ref[hi : hi + 1, :]
            scr_ref[side, pl.ds(hi, half, stride=high), :] = piece
    gate_ref[:, step * per * LANES : (step + 1) * per * LANES] = sigmoid(dot(gate_w, normed))


def flush(scr_ref, send_ref):
    parts = send_ref.shape[0]
    for side in range(2):
        send_ref[:, side] = scr_ref[side].reshape(parts, -1, LANES).astype(BF16)


def finish(step, per, tri_ref, gate_ref, base_ref, final_w):
    high = tri_ref.shape[0] // final_w.shape[1]
    rows = final_w.shape[1]
    triangle = jnp.concatenate(
        [tri_ref[pl.ds(step * per + u, rows, stride=high), :] for u in range(per)], axis=1
    )
    update = dot(final_w, norm_rows(triangle))
    span = slice(step * per * LANES, (step + 1) * per * LANES)
    return base_ref[:, span].astype(F32) + gate_ref[:, span] * update


def open_kernel(per, groups, x_ref, mask_ref, lw_ref, rw_ref, gw_ref, send_ref, gate_ref, base_ref, lane_ref, scr_ref):
    rows, width, channels = x_ref.shape
    high = rows // groups
    lane_mask(mask_ref, lane_ref, groups)
    left_w, right_w, gate_w = lw_ref[...].T, rw_ref[...].T, gw_ref[...].T
    for step in range(high // per):
        tokens = [x_ref[lo * high + step * per + u] for u in range(per) for lo in range(groups)]
        values = jnp.concatenate([t.astype(F32) for t in tokens], axis=0).T
        base_ref[:, step * per * LANES : (step + 1) * per * LANES] = values.astype(BF16)
        project(norm_rows(values), step, per, left_w, right_w, gate_w, lane_ref, scr_ref, gate_ref)
    flush(scr_ref, send_ref)


def middle_kernel(per, groups, back_ref, gate0_ref, base0_ref, fw_ref, mask_ref, lw_ref, rw_ref, gw_ref,
                  send_ref, gate_ref, base_ref, lane_ref, scr_ref, tri_ref):
    lane_mask(mask_ref, lane_ref, groups)
    tri_ref[...] = back_ref[...].reshape(tri_ref.shape).astype(F32)
    final_w = fw_ref[...].T
    left_w, right_w, gate_w = lw_ref[...].T, rw_ref[...].T, gw_ref[...].T
    for step in range(lane_ref.shape[0] // per):
        middle = finish(step, per, tri_ref, gate0_ref, base0_ref, final_w).astype(BF16)
        base_ref[:, step * per * LANES : (step + 1) * per * LANES] = middle
        project(norm_rows(middle.astype(F32)), step, per, left_w, right_w, gate_w, lane_ref, scr_ref, gate_ref)
    flush(scr_ref, send_ref)


def close_kernel(per, groups, back_ref, gate_ref, base_ref, fw_ref, inw_ref, outw_ref, out_ref, tri_ref):
    rows, width, channels = out_ref.shape
    high = rows // groups
    tri_ref[...] = back_ref[...].reshape(tri_ref.shape).astype(F32)
    final_w, in_w, out_w = fw_ref[...].T, inw_ref[...].T, outw_ref[...].T
    half = in_w.shape[0] // 2
    for step in range(high // per):
        after = finish(step, per, tri_ref, gate_ref, base_ref, final_w).astype(BF16).astype(F32)
        both = dot(in_w, norm_rows(after))
        swish = both[:half]
        hidden = (swish * sigmoid(swish) * both[half:]).astype(BF16)
        result = (after + dot(out_w, hidden)).T
        for u in range(per):
            for lo in range(groups):
                at = (u * groups + lo) * width
                out_ref[lo * high + step * per + u] = result[at : at + width].astype(BF16)


def triangle_kernel(side, groups, incoming, got_ref, send_ref):
    parts, _, rows, _ = got_ref.shape
    width = LANES // groups
    mine = rows // SUB
    turned = []
    for which in range(2):
        per_row = []
        for r in range(side):
            blocks = [got_ref[r * side + c, which].astype(F32) for c in range(side)]
            per_row.append(swap_groups(blocks, width))
        turned.append(per_row)
    sums = []
    for h in range(mine):
        span = slice(h * SUB, (h + 1) * SUB)
        left = jnp.concatenate([turned[0][r][lo][span] for lo in range(groups) for r in range(side)], axis=0).astype(BF16)
        if incoming:
            right = jnp.concatenate([turned[1][r][lo][span] for lo in range(groups) for r in range(side)], axis=0).astype(BF16)
            total = lax.dot_general(left, right, (((0,), (0,)), ((), ())), preferred_element_type=F32)
            pick = lambda r, lo: (r * groups + lo) * SUB
        else:
            right = jnp.concatenate([turned[1][r][lo][span] for r in range(side) for lo in range(groups)], axis=0).astype(BF16)
            total = lax.dot_general(left, right, (((1,), (1,)), ((), ())), preferred_element_type=F32)
            pick = lambda r, lo: (lo * side + r) * SUB
        sums.append([[total[pick(r, lo) : pick(r, lo) + SUB] for lo in range(groups)] for r in range(side)])
    for r in range(side):
        blocks = [jnp.concatenate([sums[h][r][lo] for h in range(mine)], axis=0) for lo in range(groups)]
        for c, block in enumerate(swap_groups(blocks, width)):
            send_ref[r * side + c] = block.astype(BF16)


def channel_split(side, *args):
    (x, mask, out_left_w, out_right_w, out_gate_w, out_final_w, in_left_w, in_right_w, in_gate_w, in_final_w,
     trans_in_w, trans_out_w) = args
    axes = ("row", "col")
    rows, width, channels = x.shape
    hidden = out_final_w.shape[0]
    groups = LANES // width
    high = rows // groups
    parts = side * side
    tokens = rows * width
    block = hidden // parts * high
    per = 2
    shape = jax.ShapeDtypeStruct
    send = shape((parts, 2, block, LANES), BF16)
    back = shape((parts, block, LANES), BF16)
    gate = shape((channels, tokens), F32)
    base = shape((channels, tokens), BF16)
    lane_scr = pltpu.VMEM((high, LANES), F32)
    scr = pltpu.VMEM((2, hidden * high, LANES), F32)
    tri_scr = pltpu.VMEM((hidden * high, LANES), F32)

    def exchange(values):
        return lax.all_to_all(values, axes, split_axis=0, concat_axis=0, tiled=True)

    def triangle(got, incoming, name):
        return pl.pallas_call(functools.partial(triangle_kernel, side, groups, incoming), out_shape=back, name=name)(got)

    sent, gate_out, base_out = pl.pallas_call(
        functools.partial(open_kernel, per, groups), out_shape=(send, gate, base), scratch_shapes=[lane_scr, scr], name="open"
    )(x, mask, out_left_w, out_right_w, out_gate_w)
    returned = exchange(triangle(exchange(sent), False, "outgoing"))
    sent, gate_in, base_in = pl.pallas_call(
        functools.partial(middle_kernel, per, groups), out_shape=(send, gate, base),
        scratch_shapes=[lane_scr, scr, tri_scr], name="middle",
    )(returned, gate_out, base_out, out_final_w, mask, in_left_w, in_right_w, in_gate_w)
    returned = exchange(triangle(exchange(sent), True, "incoming"))
    return pl.pallas_call(
        functools.partial(close_kernel, per, groups), out_shape=shape(x.shape, BF16), scratch_shapes=[tri_scr], name="close"
    )(returned, gate_in, base_in, in_final_w, trans_in_w, trans_out_w)


def layer_norm(values):
    average = jnp.mean(values, axis=-1, keepdims=True)
    centered = values - average
    spread = jnp.mean(centered * centered, axis=-1, keepdims=True)
    return centered * lax.rsqrt(spread + epsilon)


def gated(normed, weight, mask_vals):
    projected = jnp.dot(normed, weight, preferred_element_type=F32)
    half_width = weight.shape[1] // 2
    result = jax.nn.sigmoid(projected[..., :half_width]) * projected[..., half_width:]
    result = result * mask_vals[..., None]
    return result.astype(BF16)


def finish_plain(pair_repr, normed, triangle, gate_w, final_w):
    gate_vals = jax.nn.sigmoid(jnp.dot(normed, gate_w, preferred_element_type=F32))
    tri_norm = layer_norm(triangle).astype(BF16)
    update = jnp.dot(tri_norm, final_w, preferred_element_type=F32)
    return (pair_repr.astype(F32) + gate_vals * update).astype(BF16)


def gathers(pair_repr, pair_mask, out_left_w, out_right_w, out_gate_w, out_final_w, in_left_w, in_right_w, in_gate_w,
            in_final_w, trans_in_w, trans_out_w):
    mask_vals = pair_mask.astype(F32)
    normed_out = layer_norm(pair_repr.astype(F32)).astype(BF16)
    outbound = gated(normed_out, out_right_w, mask_vals)
    turned_right = lax.all_to_all(
        lax.all_to_all(outbound, "row", split_axis=0, concat_axis=0, tiled=True),
        "col", split_axis=0, concat_axis=1, tiled=True,
    )
    left_tile = gated(normed_out, out_left_w, mask_vals)
    gathered = lax.all_gather(left_tile, "col", axis=1, tiled=True)
    triangle = jnp.einsum(
        "ikh,jkh->ijh", gathered, lax.all_gather(turned_right, "row", axis=0, tiled=True), preferred_element_type=F32
    )
    middle = finish_plain(pair_repr, normed_out, triangle, out_gate_w, out_final_w)
    normed_in = layer_norm(middle.astype(F32)).astype(BF16)
    outbound_left = gated(normed_in, in_left_w, mask_vals)
    turned_left = lax.all_to_all(
        lax.all_to_all(outbound_left, "col", split_axis=1, concat_axis=1, tiled=True),
        "row", split_axis=1, concat_axis=0, tiled=True,
    )
    right_tile = gated(normed_in, in_right_w, mask_vals)
    column_panel = lax.all_gather(right_tile, "row", axis=0, tiled=True)
    triangle_in = jnp.einsum(
        "kih,kjh->ijh", lax.all_gather(turned_left, "col", axis=1, tiled=True), column_panel, preferred_element_type=F32
    )
    after_in = finish_plain(middle, normed_in, triangle_in, in_gate_w, in_final_w)
    normed_mix = layer_norm(after_in.astype(F32)).astype(BF16)
    projected = jnp.dot(normed_mix, trans_in_w, preferred_element_type=F32)
    half_width = trans_in_w.shape[1] // 2
    hidden = (jax.nn.silu(projected[..., :half_width]) * projected[..., half_width:]).astype(BF16)
    result = after_in.astype(F32) + jnp.dot(hidden, trans_out_w, preferred_element_type=F32)
    return result.astype(BF16)


def shards(row_size, col_size, *args):
    rows, width, channels = args[0].shape
    hidden = args[5].shape[0]
    fits = (
        row_size == col_size
        and rows == width
        and row_size * rows == LANES
        and rows % (LANES // width) == 0
        and rows // (LANES // width) == SUB
        and hidden % (row_size * col_size) == 0
        and channels == LANES
        and hidden == LANES
    )
    if fits:
        return channel_split(row_size, *args)
    return gathers(*args)


def solution(mesh):
    tile = P(("crop", "row"), "col")
    in_specs = (P(("crop", "row"), "col", None), tile) + (P(),) * 10
    out_specs = P(("crop", "row"), "col", None)
    body = functools.partial(shards, mesh.shape["row"], mesh.shape["col"])
    return jax.shard_map(body, mesh=mesh, in_specs=in_specs, out_specs=out_specs, check_vma=False)
```

time: 163 us -> 88.7 us (0.54)
  waiting for transfers between devices: 59 us -> 0 us
  Pallas kernels: 0 us -> 17.6 us
  blocking collectives: 53.1 us -> 70.4 us
  local copies, waits for them, and re-layouts: 14 us -> 0 us
  matrix products: 13.4 us -> 0 us
  between operations: 13.4 us -> 0.01 us
  other arithmetic: 8.94 us -> 0 us
    all_gather x4 -> x0, waiting for transfers between devices: 59 us -> none  [the longest x1 27.7 us: shards(): lax.all_gather(turned_left, 'col', axis=1, tiled=True)]
    pallas_call x0 -> x5, Pallas kernels: none -> 17.6 us  [the longest x2 6.03 us: triangle(): pl.pallas_call(functools.partial(triangle_kernel, side, groups, incoming)...]
    all_to_all x4, blocking collectives: 53.1 us -> 70.4 us  [exchange(): return lax.all_to_all(values, axes, split_axis=0, concat_axis=0, tiled=True)]
    dot_general x12 -> x0, matrix products: 13.4 us -> none  [the longest x4 3.27 us: gated(): projected = jnp.dot(normed, weight, preferred_element_type=jnp.float32)]
    all_gather x2 -> x0, local copies, waits for them, and re-layouts: 5.87 us -> none  [the longest x1 3.2 us: shards(): column_panel = lax.all_gather(right_tile, 'row', axis=0, tiled=True)]
    convert_element_type x3 -> x0, local copies, waits for them, and re-layouts: 5.38 us -> none  [the longest x2 5.27 us: finish(): tri_norm = layer_norm(triangle).astype(jnp.bfloat16)]
    convert_element_type x6 -> x0, other arithmetic: 4.89 us -> none  [the longest x2 2.52 us: finish(): tri_norm = layer_norm(triangle).astype(jnp.bfloat16)]
    reduce_sum x6 -> x0, other arithmetic: 3.97 us -> none  [the longest x5 2.75 us: layer_norm(): spread = jnp.mean(centered * centered, axis=-1, keepdims=True)]
  transfers between devices with their start and end apart: 4 -> 0, of which waited for: 4 -> 0; matrix products, arithmetic and copies ran while one was open for 6% -> 0% of each run, Pallas kernels for 0% -> 0%
where the time goes in v1:
time: 88.7 us; the launch traced here: 88 us
  blocking collectives  70.4 us (79%)
  Pallas kernels  17.6 us (20%)
    all_to_all x4, blocking collectives, exchange(): return lax.all_to_all(values, axes, split_axis=0, concat_axis=0, tiled=True)  70.4 us
    pallas_call x2, Pallas kernels, triangle(): pl.pallas_call(functools.partial(triangle_kernel, side, groups, incoming)...  6.03 us
    pallas_call x1, Pallas kernels, channel_split(): pl.pallas_call(functools.partial(close_kernel, per, groups), out_shape=sh...  4.88 us
    pallas_call x1, Pallas kernels, channel_split(): pl.pallas_call(functools.partial(middle_kernel, per, groups), out_shape=(...  3.88 us
    pallas_call x1, Pallas kernels, channel_split(): pl.pallas_call(functools.partial(open_kernel, per, groups), out_shape=(se...  2.84 us

profile of v1, /device:TPU:0, one launch (start us, length us, event | category | flops | bytes accessed | tf_op | source)
XLA Modules:
  0.0 88.0 jit_solution(16296742407501161569)
XLA Ops:
  0.0 2.8 %open.1 = (bf16[16,2,64,128]{3,2,1,0:T(8,128)(2,1)}, f32[128,1024]{1,0:T(8,128)}, bf16[128,1024]{1,0:T(8,128)(2,1)}) custom-call(bf16[32,32,128]{2,1,0:T(8,128)(2,1)} %x_ref.1, s32[32,32]{1,0:T(8,128)} %mask_ref.3, bf16[128,256]{1,0:T(8,128)(2,1)} %lw_ref.2, bf16[128,256]{1,0:T(8,128)(2,1)} %rw_ref.2, bf16[128,128]{1,0:T(8,128)(2,1)} %gw_ref.2), custom_call_target="tpu_custom_call" | custom-call | tf_op jit(solution)/shard_map/open/pallas_call | solution.py:186
  2.8 24.6 %all_to_all.20.got_ref = bf16[16,2,64,128]{3,2,1,0:T(8,128)(2,1)} all-to-all(bf16[16,2,64,128]{3,2,1,0:T(8,128)(2,1)} %get-tuple-element.11), channel_id=1, replica_groups=mesh['row'=4,'col'=4,'crop'=2] {'row','col'}, dimensions={0} | all-to-all | bytes 1048576 | tf_op jit(solution)/shard_map/all_to_all | solution.py:181
  27.5 2.9 %outgoing.1 = bf16[16,64,128]{2,1,0:T(8,128)(2,1)} custom-call(bf16[16,2,64,128]{3,2,1,0:T(8,128)(2,1)} %all_to_all.20.got_ref), custom_call_target="tpu_custom_call" | custom-call | tf_op jit(solution)/shard_map/outgoing/pallas_call | solution.py:184
  30.4 14.0 %all_to_all.21.back_ref = bf16[16,64,128]{2,1,0:T(8,128)(2,1)} all-to-all(bf16[16,64,128]{2,1,0:T(8,128)(2,1)} %outgoing.1), channel_id=1, replica_groups=mesh['row'=4,'col'=4,'crop'=2] {'row','col'}, dimensions={0} | all-to-all | bytes 524288 | tf_op jit(solution)/shard_map/all_to_all | solution.py:181
  44.4 3.9 %middle.1 = (bf16[16,2,64,128]{3,2,1,0:T(8,128)(2,1)}, f32[128,1024]{1,0:T(8,128)}, bf16[128,1024]{1,0:T(8,128)(2,1)}) custom-call(bf16[16,64,128]{2,1,0:T(8,128)(2,1)} %all_to_all.21.back_ref, f32[128,1024]{1,0:T(8,128)} %get-tuple-element.12.gate0_ref, bf16[128,1024]{1,0:T(8,128)(2,1)} %get-tuple-element.13.base0_ref, bf16[128,128]{1,0:T(8,128)(2,1)} %fw_ref.2, ...), custom_call_target="tpu_custom_call" | custom-call | tf_op jit(solution)/shard_map/middle/pallas_call | solution.py:190
  48.3 18.4 %all_to_all.22.got_ref = bf16[16,2,64,128]{3,2,1,0:T(8,128)(2,1)} all-to-all(bf16[16,2,64,128]{3,2,1,0:T(8,128)(2,1)} %get-tuple-element.14), channel_id=1, replica_groups=mesh['row'=4,'col'=4,'crop'=2] {'row','col'}, dimensions={0} | all-to-all | bytes 1048576 | tf_op jit(solution)/shard_map/all_to_all | solution.py:181
  66.7 3.1 %incoming.1 = bf16[16,64,128]{2,1,0:T(8,128)(2,1)} custom-call(bf16[16,2,64,128]{3,2,1,0:T(8,128)(2,1)} %all_to_all.22.got_ref), custom_call_target="tpu_custom_call" | custom-call | tf_op jit(solution)/shard_map/incoming/pallas_call | solution.py:184
  69.8 13.4 %all_to_all.23.back_ref = bf16[16,64,128]{2,1,0:T(8,128)(2,1)} all-to-all(bf16[16,64,128]{2,1,0:T(8,128)(2,1)} %incoming.1), channel_id=1, replica_groups=mesh['row'=4,'col'=4,'crop'=2] {'row','col'}, dimensions={0} | all-to-all | bytes 524288 | tf_op jit(solution)/shard_map/all_to_all | solution.py:181
  83.1 4.9 %close.1 = bf16[32,32,128]{2,1,0:T(8,128)(2,1)} custom-call(bf16[16,64,128]{2,1,0:T(8,128)(2,1)} %all_to_all.23.back_ref, f32[128,1024]{1,0:T(8,128)} %get-tuple-element.15.gate_ref, bf16[128,1024]{1,0:T(8,128)(2,1)} %get-tuple-element.16.base_ref, bf16[128,128]{1,0:T(8,128)(2,1)} %fw_ref.3, bf16[128,1024]{1,0:T(8,128)(2,1)} %inw_ref.1, ...), custom_call_target="tpu_custom_call" | custom-call | tf_op jit(solution)/shard_map/close/pallas_call | solution.py:195

commit v2 on v1

--- a/solution.py
+++ b/solution.py
@@ -11,6 +11,7 @@
 LANES = 128
 SUB = 8
 F32, BF16 = jnp.float32, jnp.bfloat16
+PARAMS = pltpu.CompilerParams(vmem_limit_bytes=16 * 1024 * 1024)
 
 
 def norm_rows(values):
@@ -181,19 +182,19 @@
         return lax.all_to_all(values, axes, split_axis=0, concat_axis=0, tiled=True)
 
     def triangle(got, incoming, name):
-        return pl.pallas_call(functools.partial(triangle_kernel, side, groups, incoming), out_shape=back, name=name)(got)
+        return pl.pallas_call(functools.partial(triangle_kernel, side, groups, incoming), out_shape=back, name=name, compiler_params=PARAMS)(got)
 
     sent, gate_out, base_out = pl.pallas_call(
-        functools.partial(open_kernel, per, groups), out_shape=(send, gate, base), scratch_shapes=[lane_scr, scr], name="open"
+        functools.partial(open_kernel, per, groups), out_shape=(send, gate, base), scratch_shapes=[lane_scr, scr], name="open", compiler_params=PARAMS
     )(x, mask, out_left_w, out_right_w, out_gate_w)
     returned = exchange(triangle(exchange(sent), False, "outgoing"))
     sent, gate_in, base_in = pl.pallas_call(
         functools.partial(middle_kernel, per, groups), out_shape=(send, gate, base),
-        scratch_shapes=[lane_scr, scr, tri_scr], name="middle",
+        scratch_shapes=[lane_scr, scr, tri_scr], name="middle", compiler_params=PARAMS,
     )(returned, gate_out, base_out, out_final_w, mask, in_left_w, in_right_w, in_gate_w)
     returned = exchange(triangle(exchange(sent), True, "incoming"))
     return pl.pallas_call(
-        functools.partial(close_kernel, per, groups), out_shape=shape(x.shape, BF16), scratch_shapes=[tri_scr], name="close"
+        functools.partial(close_kernel, per, groups), out_shape=shape(x.shape, BF16), scratch_shapes=[tri_scr], name="close", compiler_params=PARAMS
     )(returned, gate_in, base_in, in_final_w, trans_in_w, trans_out_w)
 
 

time: 88.7 us -> 81.4 us (0.918)
  Pallas kernels: 17.6 us -> 8.46 us
  local copies, waits for them, and re-layouts: 0 us -> 4.15 us
  blocking collectives: 70.4 us -> 68.1 us
    unnamed x0 -> x26, local copies, waits for them, and re-layouts: none -> 4.15 us
    pallas_call x2, Pallas kernels: 6.03 us -> 2.55 us  [triangle(): pl.pallas_call(functools.partial(triangle_kernel, side, groups, incoming)...]
    pallas_call x1, Pallas kernels: 3.88 us -> 1.57 us  [channel_split(): pl.pallas_call(functools.partial(middle_kernel, per, groups), out_shape=(...]
    all_to_all x4, blocking collectives: 70.4 us -> 68.1 us  [exchange(): return lax.all_to_all(values, axes, split_axis=0, concat_axis=0, tiled=True)]
    pallas_call x1, Pallas kernels: 2.84 us -> 0.77 us  [channel_split(): pl.pallas_call(functools.partial(open_kernel, per, groups), out_shape=(se...]
    pallas_call x1, Pallas kernels: 4.88 us -> 3.57 us  [channel_split(): pl.pallas_call(functools.partial(close_kernel, per, groups), out_shape=sh...]
where the time goes in v2:
time: 81.4 us; the launch traced here: 80.8 us
  blocking collectives  68.1 us (84%)
  Pallas kernels  8.46 us (10%)
  local copies, waits for them, and re-layouts  4.15 us (5%)
    all_to_all x4, blocking collectives, exchange(): return lax.all_to_all(values, axes, split_axis=0, concat_axis=0, tiled=True)  68.1 us
    unnamed x26, local copies, waits for them, and re-layouts  4.15 us
    pallas_call x1, Pallas kernels, channel_split(): pl.pallas_call(functools.partial(close_kernel, per, groups), out_shape=sh...  3.57 us
    pallas_call x2, Pallas kernels, triangle(): pl.pallas_call(functools.partial(triangle_kernel, side, groups, incoming)...  2.55 us

profile of v2, /device:TPU:0, one launch (start us, length us, event | category | flops | bytes accessed | tf_op | source)
XLA Modules:
  0.0 80.8 jit_solution(18074776909433112798)
XLA Ops:
  0.0 0.0 copy-start
  0.0 0.9 %copy-done = bf16[32,32,128]{2,1,0:T(8,128)(2,1)S(1)} copy-done((bf16[32,32,128]{2,1,0:T(8,128)(2,1)S(1)}, bf16[32,32,128]{2,1,0:T(8,128)(2,1)}, u32[]{:S(2)}) %copy-start) | copy-done | bytes 262168
  1.0 0.0 copy-start.3
  1.0 0.7 copy-done.3
  1.7 0.0 copy-start.5
  1.7 0.8 %copy-done.5 = bf16[128,256]{1,0:T(8,128)(2,1)S(1)} copy-done((bf16[128,256]{1,0:T(8,128)(2,1)S(1)}, bf16[128,256]{1,0:T(8,128)(2,1)}, u32[]{:S(2)}) %copy-start.5) | copy-done | bytes 65560
  2.5 0.0 copy-start.6
  2.5 0.8 %copy-done.6 = bf16[128,256]{1,0:T(8,128)(2,1)S(1)} copy-done((bf16[128,256]{1,0:T(8,128)(2,1)S(1)}, bf16[128,256]{1,0:T(8,128)(2,1)}, u32[]{:S(2)}) %copy-start.6) | copy-done | bytes 65560
  3.3 0.0 copy-start.9
  3.4 0.8 copy-done.9
  4.1 0.8 open.1
  4.9 24.3 %all_to_all.20.got_ref = bf16[16,2,64,128]{3,2,1,0:T(8,128)(2,1)S(1)} all-to-all(bf16[16,2,64,128]{3,2,1,0:T(8,128)(2,1)S(1)} %get-tuple-element.11), channel_id=1, replica_groups=mesh['row'=4,'col'=4,'crop'=2] {'row','col'}, dimensions={0} | all-to-all | bytes 1048576 | tf_op jit(solution)/shard_map/all_to_all | solution.py:182
  29.2 1.2 %outgoing.1 = bf16[16,64,128]{2,1,0:T(8,128)(2,1)S(1)} custom-call(bf16[16,2,64,128]{3,2,1,0:T(8,128)(2,1)S(1)} %all_to_all.20.got_ref), custom_call_target="tpu_custom_call" | custom-call | tf_op jit(solution)/shard_map/outgoing/pallas_call | solution.py:185
  30.4 0.0 copy-start.4
  30.4 0.0 copy-start.7
  30.4 0.0 copy-start.8
  30.4 0.0 copy-start.10
  30.4 0.0 copy-start.11
  30.5 13.0 %all_to_all.21.back_ref = bf16[16,64,128]{2,1,0:T(8,128)(2,1)S(1)} all-to-all(bf16[16,64,128]{2,1,0:T(8,128)(2,1)S(1)} %outgoing.1), channel_id=1, replica_groups=mesh['row'=4,'col'=4,'crop'=2] {'row','col'}, dimensions={0} | all-to-all | bytes 524288 | tf_op jit(solution)/shard_map/all_to_all | solution.py:182
  43.4 0.0 copy-done.4
  43.4 0.0 copy-done.7
  43.4 0.0 copy-done.8
  43.4 0.0 copy-done.10
  43.5 0.0 copy-done.11
  43.5 1.6 %middle.1 = (bf16[16,2,64,128]{3,2,1,0:T(8,128)(2,1)S(1)}, f32[128,1024]{1,0:T(8,128)S(1)}, bf16[128,1024]{1,0:T(8,128)(2,1)S(1)}) custom-call(bf16[16,64,128]{2,1,0:T(8,128)(2,1)S(1)} %all_to_all.21.back_ref, f32[128,1024]{1,0:T(8,128)S(1)} %get-tuple-element.12.gate0_ref, bf16[128,1024]{1,0:T(8,128)(2,1)S(1)} %get-tuple-element.13.base0_ref, ...), custom_call_target="tpu_custom_call" | custom-call | tf_op jit(solution)/shard_map/middle/pallas_call | solution.py:191
  45.0 18.1 %all_to_all.22.got_ref = bf16[16,2,64,128]{3,2,1,0:T(8,128)(2,1)S(1)} all-to-all(bf16[16,2,64,128]{3,2,1,0:T(8,128)(2,1)S(1)} %get-tuple-element.14), channel_id=1, replica_groups=mesh['row'=4,'col'=4,'crop'=2] {'row','col'}, dimensions={0} | all-to-all | bytes 1048576 | tf_op jit(solution)/shard_map/all_to_all | solution.py:182
  63.2 1.4 %incoming.1 = bf16[16,64,128]{2,1,0:T(8,128)(2,1)S(1)} custom-call(bf16[16,2,64,128]{3,2,1,0:T(8,128)(2,1)S(1)} %all_to_all.22.got_ref), custom_call_target="tpu_custom_call" | custom-call | tf_op jit(solution)/shard_map/incoming/pallas_call | solution.py:185
  64.5 0.0 copy-start.1
  64.6 0.0 copy-start.2
  64.6 0.0 copy-start.12
  64.6 12.7 %all_to_all.23.back_ref = bf16[16,64,128]{2,1,0:T(8,128)(2,1)S(1)} all-to-all(bf16[16,64,128]{2,1,0:T(8,128)(2,1)S(1)} %incoming.1), channel_id=1, replica_groups=mesh['row'=4,'col'=4,'crop'=2] {'row','col'}, dimensions={0} | all-to-all | bytes 524288 | tf_op jit(solution)/shard_map/all_to_all | solution.py:182
  77.3 0.0 copy-done.1
  77.3 0.0 copy-done.2
  77.3 0.0 copy-done.12
  77.3 3.6 %close.1 = bf16[32,32,128]{2,1,0:T(8,128)(2,1)} custom-call(bf16[16,64,128]{2,1,0:T(8,128)(2,1)S(1)} %all_to_all.23.back_ref, f32[128,1024]{1,0:T(8,128)S(1)} %get-tuple-element.15.gate_ref, bf16[128,1024]{1,0:T(8,128)(2,1)S(1)} %get-tuple-element.16.base_ref, bf16[128,128]{1,0:T(8,128)(2,1)S(1)} %copy-done.12, bf16[128,1024]{1,0:T(8,128)(2,1)S(1)} %copy-done.1, ...), custom_call_target="tpu_custom_call" | custom-call | tf_op jit(solution)/shard_map/close/pallas_call | solution.py:196
Async XLA Ops:
  0.0 0.9 %copy-start = (bf16[32,32,128]{2,1,0:T(8,128)(2,1)S(1)}, bf16[32,32,128]{2,1,0:T(8,128)(2,1)}, u32[]{:S(2)}) copy-start(bf16[32,32,128]{2,1,0:T(8,128)(2,1)} %x_ref.1) | copy-start | bytes 786436
  1.0 0.7 copy-start.3
  1.7 0.8 %copy-start.5 = (bf16[128,256]{1,0:T(8,128)(2,1)S(1)}, bf16[128,256]{1,0:T(8,128)(2,1)}, u32[]{:S(2)}) copy-start(bf16[128,256]{1,0:T(8,128)(2,1)} %lw_ref.2) | copy-start | bytes 196612
  2.5 0.8 %copy-start.6 = (bf16[128,256]{1,0:T(8,128)(2,1)S(1)}, bf16[128,256]{1,0:T(8,128)(2,1)}, u32[]{:S(2)}) copy-start(bf16[128,256]{1,0:T(8,128)(2,1)} %rw_ref.2) | copy-start | bytes 196612
  3.3 0.8 copy-start.9
  30.4 13.0 %copy-start.4 = (s32[32,32]{1,0:T(8,128)S(1)}, s32[32,32]{1,0:T(8,128)}, u32[]{:S(2)}) copy-start(s32[32,32]{1,0:T(8,128)} %mask_ref.3) | copy-start | bytes 12292
  30.4 13.0 %copy-start.7 = (bf16[128,256]{1,0:T(8,128)(2,1)S(1)}, bf16[128,256]{1,0:T(8,128)(2,1)}, u32[]{:S(2)}) copy-start(bf16[128,256]{1,0:T(8,128)(2,1)} %lw_ref.3) | copy-start | bytes 196612
  30.4 13.0 %copy-start.8 = (bf16[128,256]{1,0:T(8,128)(2,1)S(1)}, bf16[128,256]{1,0:T(8,128)(2,1)}, u32[]{:S(2)}) copy-start(bf16[128,256]{1,0:T(8,128)(2,1)} %rw_ref.3) | copy-start | bytes 196612
  30.4 13.0 %copy-start.10 = (bf16[128,128]{1,0:T(8,128)(2,1)S(1)}, bf16[128,128]{1,0:T(8,128)(2,1)}, u32[]{:S(2)}) copy-start(bf16[128,128]{1,0:T(8,128)(2,1)} %fw_ref.2) | copy-start | bytes 98308
  30.4 13.0 %copy-start.11 = (bf16[128,128]{1,0:T(8,128)(2,1)S(1)}, bf16[128,128]{1,0:T(8,128)(2,1)}, u32[]{:S(2)}) copy-start(bf16[128,128]{1,0:T(8,128)(2,1)} %gw_ref.3) | copy-start | bytes 98308
  64.5 12.7 %copy-start.1 = (bf16[128,1024]{1,0:T(8,128)(2,1)S(1)}, bf16[128,1024]{1,0:T(8,128)(2,1)}, u32[]{:S(2)}) copy-start(bf16[128,1024]{1,0:T(8,128)(2,1)} %inw_ref.1) | copy-start | bytes 786436
  64.6 12.7 %copy-start.2 = (bf16[512,128]{1,0:T(8,128)(2,1)S(1)}, bf16[512,128]{1,0:T(8,128)(2,1)}, u32[]{:S(2)}) copy-start(bf16[512,128]{1,0:T(8,128)(2,1)} %outw_ref.1) | copy-start | bytes 393220
  64.6 12.7 %copy-start.12 = (bf16[128,128]{1,0:T(8,128)(2,1)S(1)}, bf16[128,128]{1,0:T(8,128)(2,1)}, u32[]{:S(2)}) copy-start(bf16[128,128]{1,0:T(8,128)(2,1)} %fw_ref.3) | copy-start | bytes 98308

commit v3 on v2

--- a/solution.py
+++ b/solution.py
@@ -11,6 +11,7 @@
 LANES = 128
 SUB = 8
 F32, BF16 = jnp.float32, jnp.bfloat16
+OFFSET = 5000
 PARAMS = pltpu.CompilerParams(vmem_limit_bytes=16 * 1024 * 1024)
 
 
@@ -83,9 +84,23 @@
     return base_ref[:, span].astype(F32) + gate_ref[:, span] * update
 
 
-def open_kernel(per, groups, x_ref, mask_ref, lw_ref, rw_ref, gw_ref, send_ref, gate_ref, base_ref, lane_ref, scr_ref):
+def open_kernel(per, groups, *refs):
+    count = 5
+    far, refs = refs[:count], refs[count:]
+    send_ref, gate_ref, base_ref, lane_ref, scr_ref, *near, sems = refs
+    copies = [pltpu.make_async_copy(a, b, sems.at[at]) for at, (a, b) in enumerate(zip(far, near))]
+    for copy in copies:
+        copy.start()
+    x_ref, mask_ref, lw_ref, rw_ref, gw_ref = near
     rows, width, channels = x_ref.shape
     high = rows // groups
+
+    @pl.when(lax.axis_index("crop") == 0)
+    def _():
+        pl.delay(OFFSET)
+
+    for copy in copies:
+        copy.wait()
     lane_mask(mask_ref, lane_ref, groups)
     left_w, right_w, gate_w = lw_ref[...].T, rw_ref[...].T, gw_ref[...].T
     for step in range(high // per):
@@ -184,9 +199,12 @@
     def triangle(got, incoming, name):
         return pl.pallas_call(functools.partial(triangle_kernel, side, groups, incoming), out_shape=back, name=name, compiler_params=PARAMS)(got)
 
+    first = (x, mask, out_left_w, out_right_w, out_gate_w)
     sent, gate_out, base_out = pl.pallas_call(
-        functools.partial(open_kernel, per, groups), out_shape=(send, gate, base), scratch_shapes=[lane_scr, scr], name="open", compiler_params=PARAMS
-    )(x, mask, out_left_w, out_right_w, out_gate_w)
+        functools.partial(open_kernel, per, groups), out_shape=(send, gate, base), name="open", compiler_params=pltpu.CompilerParams(vmem_limit_bytes=60 * 1024 * 1024),
+        in_specs=[pl.BlockSpec(memory_space=pltpu.HBM)] * len(first),
+        scratch_shapes=[lane_scr, scr] + [pltpu.VMEM(a.shape, a.dtype) for a in first] + [pltpu.SemaphoreType.DMA((len(first),))],
+    )(*first)
     returned = exchange(triangle(exchange(sent), False, "outgoing"))
     sent, gate_in, base_in = pl.pallas_call(
         functools.partial(middle_kernel, per, groups), out_shape=(send, gate, base),

time: 81.4 us -> 74 us (0.909)
  blocking collectives: 68.1 us -> 58.8 us
  Pallas kernels: 8.46 us -> 14.6 us
  local copies, waits for them, and re-layouts: 4.15 us -> 0.06 us
    all_to_all x4, blocking collectives: 68.1 us -> 58.8 us  [exchange(): return lax.all_to_all(values, axes, split_axis=0, concat_axis=0, tiled=True)]
    pallas_call x1, Pallas kernels: 0.77 us -> 6.88 us  [channel_split(): pl.pallas_call(functools.partial(open_kernel, per, groups), out_shape=(se...]
    unnamed x26 -> x20, local copies, waits for them, and re-layouts: 4.15 us -> 0.06 us
where the time goes in v3:
time: 74 us; the launch traced here: 73.6 us
  blocking collectives  58.8 us (79%)
  Pallas kernels  14.6 us (20%)
    all_to_all x4, blocking collectives, exchange(): return lax.all_to_all(values, axes, split_axis=0, concat_axis=0, tiled=True)  58.8 us
    pallas_call x1, Pallas kernels, channel_split(): pl.pallas_call(functools.partial(open_kernel, per, groups), out_shape=(se...  6.88 us
    pallas_call x1, Pallas kernels, channel_split(): pl.pallas_call(functools.partial(close_kernel, per, groups), out_shape=sh...  3.57 us
    pallas_call x2, Pallas kernels, triangle(): pl.pallas_call(functools.partial(triangle_kernel, side, groups, incoming)...  2.55 us
    pallas_call x1, Pallas kernels, channel_split(): pl.pallas_call(functools.partial(middle_kernel, per, groups), out_shape=(...  1.57 us

profile of v3, /device:TPU:0, one launch (start us, length us, event | category | flops | bytes accessed | tf_op | source)
XLA Modules:
  0.0 73.6 jit_solution(11089266568742009861)
XLA Ops:
  0.0 6.9 %open.1 = (bf16[16,2,64,128]{3,2,1,0:T(8,128)(2,1)}, f32[128,1024]{1,0:T(8,128)}, bf16[128,1024]{1,0:T(8,128)(2,1)}) custom-call(bf16[32,32,128]{2,1,0:T(8,128)(2,1)} %refs_0_.1, s32[32,32]{1,0:T(8,128)} %mask_ref.1, bf16[128,256]{1,0:T(8,128)(2,1)} %refs_2_.1, bf16[128,256]{1,0:T(8,128)(2,1)} %refs_3_.1, bf16[128,128]{1,0:T(8,128)(2,1)} %refs_4_.1), custom_call_target="tpu_custom_call" | custom-call | tf_op jit(solution)/shard_map/open/pallas_call | solution.py:203
  6.9 20.5 %all_to_all.20.got_ref = bf16[16,2,64,128]{3,2,1,0:T(8,128)(2,1)S(1)} all-to-all(bf16[16,2,64,128]{3,2,1,0:T(8,128)(2,1)} %get-tuple-element.11), channel_id=1, replica_groups=mesh['row'=4,'col'=4,'crop'=2] {'row','col'}, dimensions={0} | all-to-all | bytes 1048576 | tf_op jit(solution)/shard_map/all_to_all | solution.py:197
  27.4 0.0 copy-start
  27.4 1.2 %outgoing.1 = bf16[16,64,128]{2,1,0:T(8,128)(2,1)S(1)} custom-call(bf16[16,2,64,128]{3,2,1,0:T(8,128)(2,1)S(1)} %all_to_all.20.got_ref), custom_call_target="tpu_custom_call" | custom-call | tf_op jit(solution)/shard_map/outgoing/pallas_call | solution.py:200
  28.6 0.0 copy-start.1
  28.6 0.0 copy-start.4
  28.6 0.0 copy-start.5
  28.6 0.0 copy-start.6
  28.7 0.0 copy-start.7
  28.7 0.0 copy-start.8
  28.7 11.6 %all_to_all.21.back_ref = bf16[16,64,128]{2,1,0:T(8,128)(2,1)S(1)} all-to-all(bf16[16,64,128]{2,1,0:T(8,128)(2,1)S(1)} %outgoing.1), channel_id=1, replica_groups=mesh['row'=4,'col'=4,'crop'=2] {'row','col'}, dimensions={0} | all-to-all | bytes 524288 | tf_op jit(solution)/shard_map/all_to_all | solution.py:197
  40.3 0.0 copy-done
  40.3 0.0 copy-done.1
  40.3 0.0 copy-done.4
  40.3 0.0 copy-done.5
  40.4 0.0 copy-done.6
  40.4 0.0 copy-done.7
  40.4 0.0 copy-done.8
  40.4 1.6 %middle.1 = (bf16[16,2,64,128]{3,2,1,0:T(8,128)(2,1)S(1)}, f32[128,1024]{1,0:T(8,128)S(1)}, bf16[128,1024]{1,0:T(8,128)(2,1)S(1)}) custom-call(bf16[16,64,128]{2,1,0:T(8,128)(2,1)S(1)} %all_to_all.21.back_ref, f32[128,1024]{1,0:T(8,128)S(1)} %copy-done, bf16[128,1024]{1,0:T(8,128)(2,1)S(1)} %copy-done.1, bf16[128,128]{1,0:T(8,128)(2,1)S(1)} %copy-done.7, ...), custom_call_target="tpu_custom_call" | custom-call | tf_op jit(solution)/shard_map/middle/pallas_call | solution.py:209
  42.0 15.0 %all_to_all.22.got_ref = bf16[16,2,64,128]{3,2,1,0:T(8,128)(2,1)S(1)} all-to-all(bf16[16,2,64,128]{3,2,1,0:T(8,128)(2,1)S(1)} %get-tuple-element.14), channel_id=1, replica_groups=mesh['row'=4,'col'=4,'crop'=2] {'row','col'}, dimensions={0} | all-to-all | bytes 1048576 | tf_op jit(solution)/shard_map/all_to_all | solution.py:197
  56.9 1.4 %incoming.1 = bf16[16,64,128]{2,1,0:T(8,128)(2,1)S(1)} custom-call(bf16[16,2,64,128]{3,2,1,0:T(8,128)(2,1)S(1)} %all_to_all.22.got_ref), custom_call_target="tpu_custom_call" | custom-call | tf_op jit(solution)/shard_map/incoming/pallas_call | solution.py:200
  58.3 0.0 copy-start.2
  58.3 0.0 copy-start.3
  58.4 0.0 copy-start.9
  58.4 11.7 %all_to_all.23.back_ref = bf16[16,64,128]{2,1,0:T(8,128)(2,1)S(1)} all-to-all(bf16[16,64,128]{2,1,0:T(8,128)(2,1)S(1)} %incoming.1), channel_id=1, replica_groups=mesh['row'=4,'col'=4,'crop'=2] {'row','col'}, dimensions={0} | all-to-all | bytes 524288 | tf_op jit(solution)/shard_map/all_to_all | solution.py:197
  70.0 0.0 copy-done.2
  70.0 0.0 copy-done.3
  70.0 0.0 copy-done.9
  70.0 3.6 %close.1 = bf16[32,32,128]{2,1,0:T(8,128)(2,1)} custom-call(bf16[16,64,128]{2,1,0:T(8,128)(2,1)S(1)} %all_to_all.23.back_ref, f32[128,1024]{1,0:T(8,128)S(1)} %get-tuple-element.15.gate_ref, bf16[128,1024]{1,0:T(8,128)(2,1)S(1)} %get-tuple-element.16.base_ref, bf16[128,128]{1,0:T(8,128)(2,1)S(1)} %copy-done.9, bf16[128,1024]{1,0:T(8,128)(2,1)S(1)} %copy-done.2, ...), custom_call_target="tpu_custom_call" | custom-call | tf_op jit(solution)/shard_map/close/pallas_call | solution.py:214
Async XLA Ops:
  27.4 12.9 %copy-start = (f32[128,1024]{1,0:T(8,128)S(1)}, f32[128,1024]{1,0:T(8,128)}, u32[]{:S(2)}) copy-start(f32[128,1024]{1,0:T(8,128)} %get-tuple-element.12.gate0_ref) | copy-start | bytes 1572868
  28.6 11.7 %copy-start.1 = (bf16[128,1024]{1,0:T(8,128)(2,1)S(1)}, bf16[128,1024]{1,0:T(8,128)(2,1)}, u32[]{:S(2)}) copy-start(bf16[128,1024]{1,0:T(8,128)(2,1)} %get-tuple-element.13.base0_ref) | copy-start | bytes 786436
  28.6 11.7 %copy-start.4 = (s32[32,32]{1,0:T(8,128)S(1)}, s32[32,32]{1,0:T(8,128)}, u32[]{:S(2)}) copy-start(s32[32,32]{1,0:T(8,128)} %mask_ref.1) | copy-start | bytes 12292
  28.6 11.7 %copy-start.5 = (bf16[128,256]{1,0:T(8,128)(2,1)S(1)}, bf16[128,256]{1,0:T(8,128)(2,1)}, u32[]{:S(2)}) copy-start(bf16[128,256]{1,0:T(8,128)(2,1)} %lw_ref.1) | copy-start | bytes 196612
  28.6 11.7 %copy-start.6 = (bf16[128,256]{1,0:T(8,128)(2,1)S(1)}, bf16[128,256]{1,0:T(8,128)(2,1)}, u32[]{:S(2)}) copy-start(bf16[128,256]{1,0:T(8,128)(2,1)} %rw_ref.1) | copy-start | bytes 196612
  28.7 11.7 %copy-start.7 = (bf16[128,128]{1,0:T(8,128)(2,1)S(1)}, bf16[128,128]{1,0:T(8,128)(2,1)}, u32[]{:S(2)}) copy-start(bf16[128,128]{1,0:T(8,128)(2,1)} %fw_ref.2) | copy-start | bytes 98308
  28.7 11.7 %copy-start.8 = (bf16[128,128]{1,0:T(8,128)(2,1)S(1)}, bf16[128,128]{1,0:T(8,128)(2,1)}, u32[]{:S(2)}) copy-start(bf16[128,128]{1,0:T(8,128)(2,1)} %gw_ref.1) | copy-start | bytes 98308
  58.3 11.7 %copy-start.2 = (bf16[128,1024]{1,0:T(8,128)(2,1)S(1)}, bf16[128,1024]{1,0:T(8,128)(2,1)}, u32[]{:S(2)}) copy-start(bf16[128,1024]{1,0:T(8,128)(2,1)} %inw_ref.1) | copy-start | bytes 786436
  58.3 11.7 %copy-start.3 = (bf16[512,128]{1,0:T(8,128)(2,1)S(1)}, bf16[512,128]{1,0:T(8,128)(2,1)}, u32[]{:S(2)}) copy-start(bf16[512,128]{1,0:T(8,128)(2,1)} %outw_ref.1) | copy-start | bytes 393220
  58.4 11.7 %copy-start.9 = (bf16[128,128]{1,0:T(8,128)(2,1)S(1)}, bf16[128,128]{1,0:T(8,128)(2,1)}, u32[]{:S(2)}) copy-start(bf16[128,128]{1,0:T(8,128)(2,1)} %fw_ref.3) | copy-start | bytes 98308

commit v4 on v3

--- a/solution.py
+++ b/solution.py
@@ -183,7 +183,7 @@
     parts = side * side
     tokens = rows * width
     block = hidden // parts * high
-    per = 2
+    per = high
     shape = jax.ShapeDtypeStruct
     send = shape((parts, 2, block, LANES), BF16)
     back = shape((parts, block, LANES), BF16)

time: 74 us -> 72 us (0.973)
  Pallas kernels: 14.6 us -> 12.6 us
    pallas_call x1, Pallas kernels: 3.57 us -> 2.12 us  [channel_split(): pl.pallas_call(functools.partial(close_kernel, per, groups), out_shape=sh...]
where the time goes in v4:
time: 72 us; the launch traced here: 71.6 us
  blocking collectives  58.8 us (82%)
  Pallas kernels  12.6 us (18%)
    all_to_all x4, blocking collectives, exchange(): return lax.all_to_all(values, axes, split_axis=0, concat_axis=0, tiled=True)  58.8 us
    pallas_call x1, Pallas kernels, channel_split(): pl.pallas_call(functools.partial(open_kernel, per, groups), out_shape=(se...  6.84 us
    pallas_call x2, Pallas kernels, triangle(): pl.pallas_call(functools.partial(triangle_kernel, side, groups, incoming)...  2.55 us
    pallas_call x1, Pallas kernels, channel_split(): pl.pallas_call(functools.partial(close_kernel, per, groups), out_shape=sh...  2.12 us

profile of v4, /device:TPU:0, one launch (start us, length us, event | category | flops | bytes accessed | tf_op | source)
XLA Modules:
  0.0 71.6 jit_solution(9975444052416032236)
XLA Ops:
  0.0 6.8 %open.1 = (bf16[16,2,64,128]{3,2,1,0:T(8,128)(2,1)}, f32[128,1024]{1,0:T(8,128)}, bf16[128,1024]{1,0:T(8,128)(2,1)}) custom-call(bf16[32,32,128]{2,1,0:T(8,128)(2,1)} %refs_0_.1, s32[32,32]{1,0:T(8,128)} %mask_ref.1, bf16[128,256]{1,0:T(8,128)(2,1)} %refs_2_.1, bf16[128,256]{1,0:T(8,128)(2,1)} %refs_3_.1, bf16[128,128]{1,0:T(8,128)(2,1)} %refs_4_.1), custom_call_target="tpu_custom_call" | custom-call | tf_op jit(solution)/shard_map/open/pallas_call | solution.py:203
  6.8 20.5 %all_to_all.20.got_ref = bf16[16,2,64,128]{3,2,1,0:T(8,128)(2,1)S(1)} all-to-all(bf16[16,2,64,128]{3,2,1,0:T(8,128)(2,1)} %get-tuple-element.11), channel_id=1, replica_groups=mesh['row'=4,'col'=4,'crop'=2] {'row','col'}, dimensions={0} | all-to-all | bytes 1048576 | tf_op jit(solution)/shard_map/all_to_all | solution.py:197
  27.4 0.0 copy-start
  27.4 1.2 %outgoing.1 = bf16[16,64,128]{2,1,0:T(8,128)(2,1)S(1)} custom-call(bf16[16,2,64,128]{3,2,1,0:T(8,128)(2,1)S(1)} %all_to_all.20.got_ref), custom_call_target="tpu_custom_call" | custom-call | tf_op jit(solution)/shard_map/outgoing/pallas_call | solution.py:200
  28.6 0.0 copy-start.1
  28.6 0.0 copy-start.4
  28.6 0.0 copy-start.5
  28.6 0.0 copy-start.6
  28.6 0.0 copy-start.7
  28.6 0.0 copy-start.8
  28.6 11.6 %all_to_all.21.back_ref = bf16[16,64,128]{2,1,0:T(8,128)(2,1)S(1)} all-to-all(bf16[16,64,128]{2,1,0:T(8,128)(2,1)S(1)} %outgoing.1), channel_id=1, replica_groups=mesh['row'=4,'col'=4,'crop'=2] {'row','col'}, dimensions={0} | all-to-all | bytes 524288 | tf_op jit(solution)/shard_map/all_to_all | solution.py:197
  40.3 0.0 copy-done
  40.3 0.0 copy-done.1
  40.3 0.0 copy-done.4
  40.3 0.0 copy-done.5
  40.3 0.0 copy-done.6
  40.3 0.0 copy-done.7
  40.3 0.0 copy-done.8
  40.3 1.1 %middle.1 = (bf16[16,2,64,128]{3,2,1,0:T(8,128)(2,1)S(1)}, f32[128,1024]{1,0:T(8,128)S(1)}, bf16[128,1024]{1,0:T(8,128)(2,1)S(1)}) custom-call(bf16[16,64,128]{2,1,0:T(8,128)(2,1)S(1)} %all_to_all.21.back_ref, f32[128,1024]{1,0:T(8,128)S(1)} %copy-done, bf16[128,1024]{1,0:T(8,128)(2,1)S(1)} %copy-done.1, bf16[128,128]{1,0:T(8,128)(2,1)S(1)} %copy-done.7, ...), custom_call_target="tpu_custom_call" | custom-call | tf_op jit(solution)/shard_map/middle/pallas_call | solution.py:209
  41.4 15.0 %all_to_all.22.got_ref = bf16[16,2,64,128]{3,2,1,0:T(8,128)(2,1)S(1)} all-to-all(bf16[16,2,64,128]{3,2,1,0:T(8,128)(2,1)S(1)} %get-tuple-element.14), channel_id=1, replica_groups=mesh['row'=4,'col'=4,'crop'=2] {'row','col'}, dimensions={0} | all-to-all | bytes 1048576 | tf_op jit(solution)/shard_map/all_to_all | solution.py:197
  56.4 1.4 %incoming.1 = bf16[16,64,128]{2,1,0:T(8,128)(2,1)S(1)} custom-call(bf16[16,2,64,128]{3,2,1,0:T(8,128)(2,1)S(1)} %all_to_all.22.got_ref), custom_call_target="tpu_custom_call" | custom-call | tf_op jit(solution)/shard_map/incoming/pallas_call | solution.py:200
  57.8 0.0 copy-start.2
  57.8 0.0 copy-start.3
  57.8 0.0 copy-start.9
  57.8 11.7 %all_to_all.23.back_ref = bf16[16,64,128]{2,1,0:T(8,128)(2,1)S(1)} all-to-all(bf16[16,64,128]{2,1,0:T(8,128)(2,1)S(1)} %incoming.1), channel_id=1, replica_groups=mesh['row'=4,'col'=4,'crop'=2] {'row','col'}, dimensions={0} | all-to-all | bytes 524288 | tf_op jit(solution)/shard_map/all_to_all | solution.py:197
  69.5 0.0 copy-done.2
  69.5 0.0 copy-done.3
  69.5 0.0 copy-done.9
  69.5 2.1 %close.1 = bf16[32,32,128]{2,1,0:T(8,128)(2,1)} custom-call(bf16[16,64,128]{2,1,0:T(8,128)(2,1)S(1)} %all_to_all.23.back_ref, f32[128,1024]{1,0:T(8,128)S(1)} %get-tuple-element.15.gate_ref, bf16[128,1024]{1,0:T(8,128)(2,1)S(1)} %get-tuple-element.16.base_ref, bf16[128,128]{1,0:T(8,128)(2,1)S(1)} %copy-done.9, bf16[128,1024]{1,0:T(8,128)(2,1)S(1)} %copy-done.2, ...), custom_call_target="tpu_custom_call" | custom-call | tf_op jit(solution)/shard_map/close/pallas_call | solution.py:214
Async XLA Ops:
  27.4 12.9 %copy-start = (f32[128,1024]{1,0:T(8,128)S(1)}, f32[128,1024]{1,0:T(8,128)}, u32[]{:S(2)}) copy-start(f32[128,1024]{1,0:T(8,128)} %get-tuple-element.12.gate0_ref) | copy-start | bytes 1572868
  28.6 11.7 %copy-start.1 = (bf16[128,1024]{1,0:T(8,128)(2,1)S(1)}, bf16[128,1024]{1,0:T(8,128)(2,1)}, u32[]{:S(2)}) copy-start(bf16[128,1024]{1,0:T(8,128)(2,1)} %get-tuple-element.13.base0_ref) | copy-start | bytes 786436
  28.6 11.7 %copy-start.4 = (s32[32,32]{1,0:T(8,128)S(1)}, s32[32,32]{1,0:T(8,128)}, u32[]{:S(2)}) copy-start(s32[32,32]{1,0:T(8,128)} %mask_ref.1) | copy-start | bytes 12292
  28.6 11.7 %copy-start.5 = (bf16[128,256]{1,0:T(8,128)(2,1)S(1)}, bf16[128,256]{1,0:T(8,128)(2,1)}, u32[]{:S(2)}) copy-start(bf16[128,256]{1,0:T(8,128)(2,1)} %lw_ref.1) | copy-start | bytes 196612
  28.6 11.7 %copy-start.6 = (bf16[128,256]{1,0:T(8,128)(2,1)S(1)}, bf16[128,256]{1,0:T(8,128)(2,1)}, u32[]{:S(2)}) copy-start(bf16[128,256]{1,0:T(8,128)(2,1)} %rw_ref.1) | copy-start | bytes 196612
  28.6 11.7 %copy-start.7 = (bf16[128,128]{1,0:T(8,128)(2,1)S(1)}, bf16[128,128]{1,0:T(8,128)(2,1)}, u32[]{:S(2)}) copy-start(bf16[128,128]{1,0:T(8,128)(2,1)} %fw_ref.2) | copy-start | bytes 98308
  28.6 11.7 %copy-start.8 = (bf16[128,128]{1,0:T(8,128)(2,1)S(1)}, bf16[128,128]{1,0:T(8,128)(2,1)}, u32[]{:S(2)}) copy-start(bf16[128,128]{1,0:T(8,128)(2,1)} %gw_ref.1) | copy-start | bytes 98308
  57.8 11.7 %copy-start.2 = (bf16[128,1024]{1,0:T(8,128)(2,1)S(1)}, bf16[128,1024]{1,0:T(8,128)(2,1)}, u32[]{:S(2)}) copy-start(bf16[128,1024]{1,0:T(8,128)(2,1)} %inw_ref.1) | copy-start | bytes 786436
  57.8 11.7 %copy-start.3 = (bf16[512,128]{1,0:T(8,128)(2,1)S(1)}, bf16[512,128]{1,0:T(8,128)(2,1)}, u32[]{:S(2)}) copy-start(bf16[512,128]{1,0:T(8,128)(2,1)} %outw_ref.1) | copy-start | bytes 393220
  57.8 11.7 %copy-start.9 = (bf16[128,128]{1,0:T(8,128)(2,1)S(1)}, bf16[128,128]{1,0:T(8,128)(2,1)}, u32[]{:S(2)}) copy-start(bf16[128,128]{1,0:T(8,128)(2,1)} %fw_ref.3) | copy-start | bytes 98308

commit v5 on v4

--- a/solution.py
+++ b/solution.py
@@ -64,7 +64,8 @@
             hi = step * per + u
             piece = value[:, u * LANES : (u + 1) * LANES] * lane_ref[hi : hi + 1, :]
             scr_ref[side, pl.ds(hi, half, stride=high), :] = piece
-    gate_ref[:, step * per * LANES : (step + 1) * per * LANES] = sigmoid(dot(gate_w, normed))
+    if gate_ref is not None:
+        gate_ref[:, step * per * LANES : (step + 1) * per * LANES] = sigmoid(dot(gate_w, normed))
 
 
 def flush(scr_ref, send_ref):
@@ -85,13 +86,13 @@
 
 
 def open_kernel(per, groups, *refs):
-    count = 5
+    count = 4
     far, refs = refs[:count], refs[count:]
-    send_ref, gate_ref, base_ref, lane_ref, scr_ref, *near, sems = refs
+    send_ref, lane_ref, scr_ref, *near, sems = refs
     copies = [pltpu.make_async_copy(a, b, sems.at[at]) for at, (a, b) in enumerate(zip(far, near))]
     for copy in copies:
         copy.start()
-    x_ref, mask_ref, lw_ref, rw_ref, gw_ref = near
+    x_ref, mask_ref, lw_ref, rw_ref = near
     rows, width, channels = x_ref.shape
     high = rows // groups
 
@@ -102,13 +103,20 @@
     for copy in copies:
         copy.wait()
     lane_mask(mask_ref, lane_ref, groups)
-    left_w, right_w, gate_w = lw_ref[...].T, rw_ref[...].T, gw_ref[...].T
+    left_w, right_w = lw_ref[...].T, rw_ref[...].T
     for step in range(high // per):
         tokens = [x_ref[lo * high + step * per + u] for u in range(per) for lo in range(groups)]
         values = jnp.concatenate([t.astype(F32) for t in tokens], axis=0).T
-        base_ref[:, step * per * LANES : (step + 1) * per * LANES] = values.astype(BF16)
-        project(norm_rows(values), step, per, left_w, right_w, gate_w, lane_ref, scr_ref, gate_ref)
+        project(norm_rows(values), step, per, left_w, right_w, None, lane_ref, scr_ref, None)
     flush(scr_ref, send_ref)
+
+
+def gate_kernel(groups, x_ref, gw_ref, gate_ref, base_ref):
+    high = x_ref.shape[0] // groups
+    tokens = [x_ref[lo * high + u] for u in range(high) for lo in range(groups)]
+    values = jnp.concatenate([t.astype(F32) for t in tokens], axis=0).T
+    base_ref[...] = values.astype(BF16)
+    gate_ref[...] = sigmoid(dot(gw_ref[...].T, norm_rows(values)))
 
 
 def middle_kernel(per, groups, back_ref, gate0_ref, base0_ref, fw_ref, mask_ref, lw_ref, rw_ref, gw_ref,
@@ -150,26 +158,26 @@
     for which in range(2):
         per_row = []
         for r in range(side):
-            blocks = [got_ref[r * side + c, which].astype(F32) for c in range(side)]
+            blocks = [got_ref[r * side + c, which] for c in range(side)]
             per_row.append(swap_groups(blocks, width))
         turned.append(per_row)
     sums = []
     for h in range(mine):
         span = slice(h * SUB, (h + 1) * SUB)
-        left = jnp.concatenate([turned[0][r][lo][span] for lo in range(groups) for r in range(side)], axis=0).astype(BF16)
+        left = jnp.concatenate([turned[0][r][lo][span] for lo in range(groups) for r in range(side)], axis=0)
         if incoming:
-            right = jnp.concatenate([turned[1][r][lo][span] for lo in range(groups) for r in range(side)], axis=0).astype(BF16)
+            right = jnp.concatenate([turned[1][r][lo][span] for lo in range(groups) for r in range(side)], axis=0)
             total = lax.dot_general(left, right, (((0,), (0,)), ((), ())), preferred_element_type=F32)
             pick = lambda r, lo: (r * groups + lo) * SUB
         else:
-            right = jnp.concatenate([turned[1][r][lo][span] for r in range(side) for lo in range(groups)], axis=0).astype(BF16)
+            right = jnp.concatenate([turned[1][r][lo][span] for r in range(side) for lo in range(groups)], axis=0)
             total = lax.dot_general(left, right, (((1,), (1,)), ((), ())), preferred_element_type=F32)
             pick = lambda r, lo: (lo * side + r) * SUB
         sums.append([[total[pick(r, lo) : pick(r, lo) + SUB] for lo in range(groups)] for r in range(side)])
     for r in range(side):
-        blocks = [jnp.concatenate([sums[h][r][lo] for h in range(mine)], axis=0) for lo in range(groups)]
+        blocks = [jnp.concatenate([sums[h][r][lo] for h in range(mine)], axis=0).astype(BF16) for lo in range(groups)]
         for c, block in enumerate(swap_groups(blocks, width)):
-            send_ref[r * side + c] = block.astype(BF16)
+            send_ref[r * side + c] = block
 
 
 def channel_split(side, *args):
@@ -199,13 +207,18 @@
     def triangle(got, incoming, name):
         return pl.pallas_call(functools.partial(triangle_kernel, side, groups, incoming), out_shape=back, name=name, compiler_params=PARAMS)(got)
 
-    first = (x, mask, out_left_w, out_right_w, out_gate_w)
-    sent, gate_out, base_out = pl.pallas_call(
-        functools.partial(open_kernel, per, groups), out_shape=(send, gate, base), name="open", compiler_params=pltpu.CompilerParams(vmem_limit_bytes=60 * 1024 * 1024),
+    first = (x, mask, out_left_w, out_right_w)
+    sent = pl.pallas_call(
+        functools.partial(open_kernel, per, groups), out_shape=send, name="open", compiler_params=pltpu.CompilerParams(vmem_limit_bytes=60 * 1024 * 1024),
         in_specs=[pl.BlockSpec(memory_space=pltpu.HBM)] * len(first),
         scratch_shapes=[lane_scr, scr] + [pltpu.VMEM(a.shape, a.dtype) for a in first] + [pltpu.SemaphoreType.DMA((len(first),))],
     )(*first)
-    returned = exchange(triangle(exchange(sent), False, "outgoing"))
+    gate_out, base_out = pl.pallas_call(
+        functools.partial(gate_kernel, groups), out_shape=(gate, base), name="gate", compiler_params=PARAMS,
+        cost_estimate=pl.CostEstimate(flops=1 << 34, bytes_accessed=1 << 20, transcendentals=0),
+    )(x, out_gate_w)
+    got, gate_out, base_out = lax.optimization_barrier((exchange(sent), gate_out, base_out))
+    returned = exchange(triangle(got, False, "outgoing"))
     sent, gate_in, base_in = pl.pallas_call(
         functools.partial(middle_kernel, per, groups), out_shape=(send, gate, base),
         scratch_shapes=[lane_scr, scr, tri_scr], name="middle", compiler_params=PARAMS,

time: 72 us -> 71.1 us (0.987)
  blocking collectives: 58.8 us -> 38.3 us
  waiting for transfers between devices: 0 us -> 11.7 us
  starting transfers between devices: 0 us -> 8.48 us
    all_to_all x4 -> x3, blocking collectives: 58.8 us -> 38.3 us  [exchange(): return lax.all_to_all(values, axes, split_axis=0, concat_axis=0, tiled=True)]
    all_to_all x0 -> x1, waiting for transfers between devices: none -> 11.7 us  [exchange(): return lax.all_to_all(values, axes, split_axis=0, concat_axis=0, tiled=True)]
    all_to_all x0 -> x1, starting transfers between devices: none -> 8.48 us  [exchange(): return lax.all_to_all(values, axes, split_axis=0, concat_axis=0, tiled=True)]
    pallas_call x2, Pallas kernels: 2.55 us -> 1.78 us  [triangle(): pl.pallas_call(functools.partial(triangle_kernel, side, groups, incoming)...]
    pallas_call x1 -> x2, Pallas kernels: 6.84 us -> 7 us  [the longest x1 6.55 us: channel_split(): pl.pallas_call(functools.partial(open_kernel, per, groups), out_shape=sen...]
  transfers between devices with their start and end apart: 0 -> 1, of which waited for: 0 -> 1; matrix products, arithmetic and copies ran while one was open for 0% -> 0% of each run, Pallas kernels for 0% -> 1%
where the time goes in v5:
time: 71.1 us; the launch traced here: 70.7 us
  blocking collectives  38.3 us (54%)
  Pallas kernels  12 us (17%)
  waiting for transfers between devices  11.7 us (16%)
  starting transfers between devices  8.48 us (12%)
    all_to_all x3, blocking collectives, exchange(): return lax.all_to_all(values, axes, split_axis=0, concat_axis=0, tiled=True)  38.3 us
    all_to_all x1, waiting for transfers between devices, exchange(): return lax.all_to_all(values, axes, split_axis=0, concat_axis=0, tiled=True)  11.7 us
    all_to_all x1, starting transfers between devices, exchange(): return lax.all_to_all(values, axes, split_axis=0, concat_axis=0, tiled=True)  8.48 us
    pallas_call x1, Pallas kernels, channel_split(): pl.pallas_call(functools.partial(open_kernel, per, groups), out_shape=sen...  6.55 us
    pallas_call x1, Pallas kernels, channel_split(): pl.pallas_call(functools.partial(close_kernel, per, groups), out_shape=sh...  2.13 us
    pallas_call x2, Pallas kernels, triangle(): pl.pallas_call(functools.partial(triangle_kernel, side, groups, incoming)...  1.78 us
  transfers between devices with their start and end apart: 1, of which 1 were waited for; matrix products, arithmetic and copies ran while one was open for 0% of the time, Pallas kernels for 1%

profile of v5, /device:TPU:0, one launch (start us, length us, event | category | flops | bytes accessed | tf_op | source)
XLA Modules:
  0.0 70.7 jit_solution(2557239741440215934)
XLA Ops:
  0.0 6.6 %open.1 = bf16[16,2,64,128]{3,2,1,0:T(8,128)(2,1)} custom-call(bf16[32,32,128]{2,1,0:T(8,128)(2,1)} %x_ref.1, s32[32,32]{1,0:T(8,128)} %mask_ref.1, bf16[128,256]{1,0:T(8,128)(2,1)} %refs_2_.1, bf16[128,256]{1,0:T(8,128)(2,1)} %refs_3_.1), custom_call_target="tpu_custom_call" | custom-call | tf_op jit(solution)/shard_map/open/pallas_call | solution.py:211
  6.6 0.0 copy-start
  6.6 0.0 copy-start.9
  6.6 8.5 %all-to-all-start = ((bf16[16,2,64,128]{3,2,1,0:T(8,128)(2,1)}), bf16[16,2,64,128]{3,2,1,0:T(8,128)(2,1)S(1)}, u32[]{:S(2)}, u32[]{:S(2)}) async-start(bf16[16,2,64,128]{3,2,1,0:T(8,128)(2,1)} %open.1), calls=%async_computation | async-start | bytes 1048576 | tf_op jit(solution)/shard_map/all_to_all | solution.py:205
  15.1 0.0 copy-done
  15.1 0.0 copy-done.9
  15.1 0.4 gate.1
  15.6 11.7 %all-to-all-done.got_ref = bf16[16,2,64,128]{3,2,1,0:T(8,128)(2,1)S(1)} async-done(((bf16[16,2,64,128]{3,2,1,0:T(8,128)(2,1)}), bf16[16,2,64,128]{3,2,1,0:T(8,128)(2,1)S(1)}, u32[]{:S(2)}, u32[]{:S(2)}) %all-to-all-start) | async-done | bytes 524320 | tf_op jit(solution)/shard_map/all_to_all | solution.py:205
  27.3 0.7 outgoing.1
  28.0 0.0 copy-start.3
  28.0 0.0 copy-start.4
  28.0 0.0 copy-start.5
  28.0 0.0 copy-start.6
  28.0 0.0 copy-start.7
  28.0 11.6 %all_to_all.20.back_ref = bf16[16,64,128]{2,1,0:T(8,128)(2,1)S(1)} all-to-all(bf16[16,64,128]{2,1,0:T(8,128)(2,1)S(1)} %outgoing.1), channel_id=1, replica_groups=mesh['row'=4,'col'=4,'crop'=2] {'row','col'}, dimensions={0} | all-to-all | bytes 524288 | tf_op jit(solution)/shard_map/all_to_all | solution.py:205
  39.7 0.0 copy-done.3
  39.7 0.0 copy-done.4
  39.7 0.0 copy-done.5
  39.7 0.0 copy-done.6
  39.7 0.0 copy-done.7
  39.7 1.1 %middle.1 = (bf16[16,2,64,128]{3,2,1,0:T(8,128)(2,1)S(1)}, f32[128,1024]{1,0:T(8,128)S(1)}, bf16[128,1024]{1,0:T(8,128)(2,1)S(1)}) custom-call(bf16[16,64,128]{2,1,0:T(8,128)(2,1)S(1)} %all_to_all.20.back_ref, f32[128,1024]{1,0:T(8,128)S(1)} %get-tuple-element.16.gate0_ref, bf16[128,1024]{1,0:T(8,128)(2,1)S(1)} %get-tuple-element.17.base0_ref, ...), custom_call_target="tpu_custom_call" | custom-call | tf_op jit(solution)/shard_map/middle/pallas_call | solution.py:222
  40.8 15.0 %all_to_all.21.got_ref = bf16[16,2,64,128]{3,2,1,0:T(8,128)(2,1)S(1)} all-to-all(bf16[16,2,64,128]{3,2,1,0:T(8,128)(2,1)S(1)} %get-tuple-element.18), channel_id=1, replica_groups=mesh['row'=4,'col'=4,'crop'=2] {'row','col'}, dimensions={0} | all-to-all | bytes 1048576 | tf_op jit(solution)/shard_map/all_to_all | solution.py:205
  55.8 1.1 %incoming.1 = bf16[16,64,128]{2,1,0:T(8,128)(2,1)S(1)} custom-call(bf16[16,2,64,128]{3,2,1,0:T(8,128)(2,1)S(1)} %all_to_all.21.got_ref), custom_call_target="tpu_custom_call" | custom-call | tf_op jit(solution)/shard_map/incoming/pallas_call | solution.py:208
  56.9 0.0 copy-start.1
  56.9 0.0 copy-start.2
  56.9 0.0 copy-start.8
  56.9 11.7 %all_to_all.22.back_ref = bf16[16,64,128]{2,1,0:T(8,128)(2,1)S(1)} all-to-all(bf16[16,64,128]{2,1,0:T(8,128)(2,1)S(1)} %incoming.1), channel_id=1, replica_groups=mesh['row'=4,'col'=4,'crop'=2] {'row','col'}, dimensions={0} | all-to-all | bytes 524288 | tf_op jit(solution)/shard_map/all_to_all | solution.py:205
  68.6 0.0 copy-done.1
  68.6 0.0 copy-done.2
  68.6 0.0 copy-done.8
  68.6 2.1 %close.1 = bf16[32,32,128]{2,1,0:T(8,128)(2,1)} custom-call(bf16[16,64,128]{2,1,0:T(8,128)(2,1)S(1)} %all_to_all.22.back_ref, f32[128,1024]{1,0:T(8,128)S(1)} %get-tuple-element.19.gate_ref, bf16[128,1024]{1,0:T(8,128)(2,1)S(1)} %get-tuple-element.20.base_ref, bf16[128,128]{1,0:T(8,128)(2,1)S(1)} %copy-done.8, bf16[128,1024]{1,0:T(8,128)(2,1)S(1)} %copy-done.1, ...), custom_call_target="tpu_custom_call" | custom-call | tf_op jit(solution)/shard_map/close/pallas_call | solution.py:227
Async XLA Ops:
  6.6 8.5 %copy-start = (bf16[32,32,128]{2,1,0:T(8,128)(2,1)S(1)}, bf16[32,32,128]{2,1,0:T(8,128)(2,1)}, u32[]{:S(2)}) copy-start(bf16[32,32,128]{2,1,0:T(8,128)(2,1)} %x_ref.1) | copy-start | bytes 786436
  6.6 8.5 %copy-start.9 = (bf16[128,128]{1,0:T(8,128)(2,1)S(1)}, bf16[128,128]{1,0:T(8,128)(2,1)}, u32[]{:S(2)}) copy-start(bf16[128,128]{1,0:T(8,128)(2,1)} %gw_ref.2) | copy-start | bytes 98308
  6.6 20.7 %all-to-all-start = ((bf16[16,2,64,128]{3,2,1,0:T(8,128)(2,1)}), bf16[16,2,64,128]{3,2,1,0:T(8,128)(2,1)S(1)}, u32[]{:S(2)}, u32[]{:S(2)}) async-start(bf16[16,2,64,128]{3,2,1,0:T(8,128)(2,1)} %open.1), calls=%async_computation | async-start | bytes 1048576 | tf_op jit(solution)/shard_map/all_to_all | solution.py:205
  28.0 11.7 %copy-start.3 = (s32[32,32]{1,0:T(8,128)S(1)}, s32[32,32]{1,0:T(8,128)}, u32[]{:S(2)}) copy-start(s32[32,32]{1,0:T(8,128)} %mask_ref.1) | copy-start | bytes 12292
  28.0 11.7 %copy-start.4 = (bf16[128,256]{1,0:T(8,128)(2,1)S(1)}, bf16[128,256]{1,0:T(8,128)(2,1)}, u32[]{:S(2)}) copy-start(bf16[128,256]{1,0:T(8,128)(2,1)} %lw_ref.1) | copy-start | bytes 196612
  28.0 11.7 %copy-start.5 = (bf16[128,256]{1,0:T(8,128)(2,1)S(1)}, bf16[128,256]{1,0:T(8,128)(2,1)}, u32[]{:S(2)}) copy-start(bf16[128,256]{1,0:T(8,128)(2,1)} %rw_ref.1) | copy-start | bytes 196612
  28.0 11.7 %copy-start.6 = (bf16[128,128]{1,0:T(8,128)(2,1)S(1)}, bf16[128,128]{1,0:T(8,128)(2,1)}, u32[]{:S(2)}) copy-start(bf16[128,128]{1,0:T(8,128)(2,1)} %fw_ref.2) | copy-start | bytes 98308
  28.0 11.7 %copy-start.7 = (bf16[128,128]{1,0:T(8,128)(2,1)S(1)}, bf16[128,128]{1,0:T(8,128)(2,1)}, u32[]{:S(2)}) copy-start(bf16[128,128]{1,0:T(8,128)(2,1)} %gw_ref.3) | copy-start | bytes 98308
  56.9 11.7 %copy-start.1 = (bf16[128,1024]{1,0:T(8,128)(2,1)S(1)}, bf16[128,1024]{1,0:T(8,128)(2,1)}, u32[]{:S(2)}) copy-start(bf16[128,1024]{1,0:T(8,128)(2,1)} %inw_ref.1) | copy-start | bytes 786436
  56.9 11.7 %copy-start.2 = (bf16[512,128]{1,0:T(8,128)(2,1)S(1)}, bf16[512,128]{1,0:T(8,128)(2,1)}, u32[]{:S(2)}) copy-start(bf16[512,128]{1,0:T(8,128)(2,1)} %outw_ref.1) | copy-start | bytes 393220
  56.9 11.7 %copy-start.8 = (bf16[128,128]{1,0:T(8,128)(2,1)S(1)}, bf16[128,128]{1,0:T(8,128)(2,1)}, u32[]{:S(2)}) copy-start(bf16[128,128]{1,0:T(8,128)(2,1)} %fw_ref.3) | copy-start | bytes 98308

commit v6 on v5

--- a/solution.py
+++ b/solution.py
@@ -158,7 +158,7 @@
     for which in range(2):
         per_row = []
         for r in range(side):
-            blocks = [got_ref[r * side + c, which] for c in range(side)]
+            blocks = [got_ref[c * side + r, which] for c in range(side)]
             per_row.append(swap_groups(blocks, width))
         turned.append(per_row)
     sums = []
@@ -177,13 +177,13 @@
     for r in range(side):
         blocks = [jnp.concatenate([sums[h][r][lo] for h in range(mine)], axis=0).astype(BF16) for lo in range(groups)]
         for c, block in enumerate(swap_groups(blocks, width)):
-            send_ref[r * side + c] = block
+            send_ref[c * side + r] = block
 
 
 def channel_split(side, *args):
     (x, mask, out_left_w, out_right_w, out_gate_w, out_final_w, in_left_w, in_right_w, in_gate_w, in_final_w,
      trans_in_w, trans_out_w) = args
-    axes = ("row", "col")
+    axes = ("col", "row")
     rows, width, channels = x.shape
     hidden = out_final_w.shape[0]
     groups = LANES // width

time: 71.1 us -> 70.6 us (level)
  waiting for transfers between devices: 11.7 us -> 10.5 us
  blocking collectives: 38.3 us -> 39.1 us
    all_to_all x1, waiting for transfers between devices: 11.7 us -> 10.5 us  [exchange(): return lax.all_to_all(values, axes, split_axis=0, concat_axis=0, tiled=True)]
    all_to_all x3, blocking collectives: 38.3 us -> 39.1 us  [exchange(): return lax.all_to_all(values, axes, split_axis=0, concat_axis=0, tiled=True)]
where the time goes in v6:
time: 70.6 us; the launch traced here: 70.2 us
  blocking collectives  39.1 us (55%)
  Pallas kernels  12 us (17%)
  waiting for transfers between devices  10.5 us (15%)
  starting transfers between devices  8.48 us (12%)
    all_to_all x3, blocking collectives, exchange(): return lax.all_to_all(values, axes, split_axis=0, concat_axis=0, tiled=True)  39.1 us
    all_to_all x1, waiting for transfers between devices, exchange(): return lax.all_to_all(values, axes, split_axis=0, concat_axis=0, tiled=True)  10.5 us
    all_to_all x1, starting transfers between devices, exchange(): return lax.all_to_all(values, axes, split_axis=0, concat_axis=0, tiled=True)  8.48 us
    pallas_call x1, Pallas kernels, channel_split(): pl.pallas_call(functools.partial(open_kernel, per, groups), out_shape=sen...  6.55 us
    pallas_call x1, Pallas kernels, channel_split(): pl.pallas_call(functools.partial(close_kernel, per, groups), out_shape=sh...  2.13 us
    pallas_call x2, Pallas kernels, triangle(): pl.pallas_call(functools.partial(triangle_kernel, side, groups, incoming)...  1.78 us
  transfers between devices with their start and end apart: 1, of which 1 were waited for; matrix products, arithmetic and copies ran while one was open for 0% of the time, Pallas kernels for 1%

profile of v6, /device:TPU:0, one launch (start us, length us, event | category | flops | bytes accessed | tf_op | source)
XLA Modules:
  0.0 70.2 jit_solution(8373430751006337894)
XLA Ops:
  0.0 6.6 %open.1 = bf16[16,2,64,128]{3,2,1,0:T(8,128)(2,1)} custom-call(bf16[32,32,128]{2,1,0:T(8,128)(2,1)} %x_ref.1, s32[32,32]{1,0:T(8,128)} %mask_ref.1, bf16[128,256]{1,0:T(8,128)(2,1)} %refs_2_.1, bf16[128,256]{1,0:T(8,128)(2,1)} %refs_3_.1), custom_call_target="tpu_custom_call" | custom-call | tf_op jit(solution)/shard_map/open/pallas_call | solution.py:211
  6.6 0.0 copy-start
  6.6 0.0 copy-start.9
  6.6 8.5 %all-to-all-start = ((bf16[16,2,64,128]{3,2,1,0:T(8,128)(2,1)}), bf16[16,2,64,128]{3,2,1,0:T(8,128)(2,1)S(1)}, u32[]{:S(2)}, u32[]{:S(2)}) async-start(bf16[16,2,64,128]{3,2,1,0:T(8,128)(2,1)} %open.1), calls=%async_computation | async-start | bytes 1048576 | tf_op jit(solution)/shard_map/all_to_all | solution.py:205
  15.1 0.0 copy-done
  15.1 0.0 copy-done.9
  15.1 0.4 gate.1
  15.6 10.5 %all-to-all-done.got_ref = bf16[16,2,64,128]{3,2,1,0:T(8,128)(2,1)S(1)} async-done(((bf16[16,2,64,128]{3,2,1,0:T(8,128)(2,1)}), bf16[16,2,64,128]{3,2,1,0:T(8,128)(2,1)S(1)}, u32[]{:S(2)}, u32[]{:S(2)}) %all-to-all-start) | async-done | bytes 524320 | tf_op jit(solution)/shard_map/all_to_all | solution.py:205
  26.0 0.7 outgoing.1
  26.7 0.0 copy-start.3
  26.7 0.0 copy-start.4
  26.7 0.0 copy-start.5
  26.7 0.0 copy-start.6
  26.8 0.0 copy-start.7
  26.8 12.5 %all_to_all.20.back_ref = bf16[16,64,128]{2,1,0:T(8,128)(2,1)S(1)} all-to-all(bf16[16,64,128]{2,1,0:T(8,128)(2,1)S(1)} %outgoing.1), channel_id=1, replica_groups=mesh['row'=4,'col'=4,'crop'=2] {'col','row'}, dimensions={0} | all-to-all | bytes 524288 | tf_op jit(solution)/shard_map/all_to_all | solution.py:205
  39.2 0.0 copy-done.3
  39.2 0.0 copy-done.4
  39.2 0.0 copy-done.5
  39.3 0.0 copy-done.6
  39.3 0.0 copy-done.7
  39.3 1.1 %middle.1 = (bf16[16,2,64,128]{3,2,1,0:T(8,128)(2,1)S(1)}, f32[128,1024]{1,0:T(8,128)S(1)}, bf16[128,1024]{1,0:T(8,128)(2,1)S(1)}) custom-call(bf16[16,64,128]{2,1,0:T(8,128)(2,1)S(1)} %all_to_all.20.back_ref, f32[128,1024]{1,0:T(8,128)S(1)} %get-tuple-element.16.gate0_ref, bf16[128,1024]{1,0:T(8,128)(2,1)S(1)} %get-tuple-element.17.base0_ref, ...), custom_call_target="tpu_custom_call" | custom-call | tf_op jit(solution)/shard_map/middle/pallas_call | solution.py:222
  40.4 14.1 %all_to_all.21.got_ref = bf16[16,2,64,128]{3,2,1,0:T(8,128)(2,1)S(1)} all-to-all(bf16[16,2,64,128]{3,2,1,0:T(8,128)(2,1)S(1)} %get-tuple-element.18), channel_id=1, replica_groups=mesh['row'=4,'col'=4,'crop'=2] {'col','row'}, dimensions={0} | all-to-all | bytes 1048576 | tf_op jit(solution)/shard_map/all_to_all | solution.py:205
  54.5 1.1 %incoming.1 = bf16[16,64,128]{2,1,0:T(8,128)(2,1)S(1)} custom-call(bf16[16,2,64,128]{3,2,1,0:T(8,128)(2,1)S(1)} %all_to_all.21.got_ref), custom_call_target="tpu_custom_call" | custom-call | tf_op jit(solution)/shard_map/incoming/pallas_call | solution.py:208
  55.6 0.0 copy-start.1
  55.6 0.0 copy-start.2
  55.6 0.0 copy-start.8
  55.6 12.5 %all_to_all.22.back_ref = bf16[16,64,128]{2,1,0:T(8,128)(2,1)S(1)} all-to-all(bf16[16,64,128]{2,1,0:T(8,128)(2,1)S(1)} %incoming.1), channel_id=1, replica_groups=mesh['row'=4,'col'=4,'crop'=2] {'col','row'}, dimensions={0} | all-to-all | bytes 524288 | tf_op jit(solution)/shard_map/all_to_all | solution.py:205
  68.1 0.0 copy-done.1
  68.1 0.0 copy-done.2
  68.1 0.0 copy-done.8
  68.1 2.1 %close.1 = bf16[32,32,128]{2,1,0:T(8,128)(2,1)} custom-call(bf16[16,64,128]{2,1,0:T(8,128)(2,1)S(1)} %all_to_all.22.back_ref, f32[128,1024]{1,0:T(8,128)S(1)} %get-tuple-element.19.gate_ref, bf16[128,1024]{1,0:T(8,128)(2,1)S(1)} %get-tuple-element.20.base_ref, bf16[128,128]{1,0:T(8,128)(2,1)S(1)} %copy-done.8, bf16[128,1024]{1,0:T(8,128)(2,1)S(1)} %copy-done.1, ...), custom_call_target="tpu_custom_call" | custom-call | tf_op jit(solution)/shard_map/close/pallas_call | solution.py:227
Async XLA Ops:
  6.6 8.5 %copy-start = (bf16[32,32,128]{2,1,0:T(8,128)(2,1)S(1)}, bf16[32,32,128]{2,1,0:T(8,128)(2,1)}, u32[]{:S(2)}) copy-start(bf16[32,32,128]{2,1,0:T(8,128)(2,1)} %x_ref.1) | copy-start | bytes 786436
  6.6 8.5 %copy-start.9 = (bf16[128,128]{1,0:T(8,128)(2,1)S(1)}, bf16[128,128]{1,0:T(8,128)(2,1)}, u32[]{:S(2)}) copy-start(bf16[128,128]{1,0:T(8,128)(2,1)} %gw_ref.2) | copy-start | bytes 98308
  6.6 19.4 %all-to-all-start = ((bf16[16,2,64,128]{3,2,1,0:T(8,128)(2,1)}), bf16[16,2,64,128]{3,2,1,0:T(8,128)(2,1)S(1)}, u32[]{:S(2)}, u32[]{:S(2)}) async-start(bf16[16,2,64,128]{3,2,1,0:T(8,128)(2,1)} %open.1), calls=%async_computation | async-start | bytes 1048576 | tf_op jit(solution)/shard_map/all_to_all | solution.py:205
  26.7 12.5 %copy-start.3 = (s32[32,32]{1,0:T(8,128)S(1)}, s32[32,32]{1,0:T(8,128)}, u32[]{:S(2)}) copy-start(s32[32,32]{1,0:T(8,128)} %mask_ref.1) | copy-start | bytes 12292
  26.7 12.5 %copy-start.4 = (bf16[128,256]{1,0:T(8,128)(2,1)S(1)}, bf16[128,256]{1,0:T(8,128)(2,1)}, u32[]{:S(2)}) copy-start(bf16[128,256]{1,0:T(8,128)(2,1)} %lw_ref.1) | copy-start | bytes 196612
  26.7 12.5 %copy-start.5 = (bf16[128,256]{1,0:T(8,128)(2,1)S(1)}, bf16[128,256]{1,0:T(8,128)(2,1)}, u32[]{:S(2)}) copy-start(bf16[128,256]{1,0:T(8,128)(2,1)} %rw_ref.1) | copy-start | bytes 196612
  26.7 12.5 %copy-start.6 = (bf16[128,128]{1,0:T(8,128)(2,1)S(1)}, bf16[128,128]{1,0:T(8,128)(2,1)}, u32[]{:S(2)}) copy-start(bf16[128,128]{1,0:T(8,128)(2,1)} %fw_ref.2) | copy-start | bytes 98308
  26.8 12.5 %copy-start.7 = (bf16[128,128]{1,0:T(8,128)(2,1)S(1)}, bf16[128,128]{1,0:T(8,128)(2,1)}, u32[]{:S(2)}) copy-start(bf16[128,128]{1,0:T(8,128)(2,1)} %gw_ref.3) | copy-start | bytes 98308
  55.6 12.5 %copy-start.1 = (bf16[128,1024]{1,0:T(8,128)(2,1)S(1)}, bf16[128,1024]{1,0:T(8,128)(2,1)}, u32[]{:S(2)}) copy-start(bf16[128,1024]{1,0:T(8,128)(2,1)} %inw_ref.1) | copy-start | bytes 786436
  55.6 12.5 %copy-start.2 = (bf16[512,128]{1,0:T(8,128)(2,1)S(1)}, bf16[512,128]{1,0:T(8,128)(2,1)}, u32[]{:S(2)}) copy-start(bf16[512,128]{1,0:T(8,128)(2,1)} %outw_ref.1) | copy-start | bytes 393220
  55.6 12.5 %copy-start.8 = (bf16[128,128]{1,0:T(8,128)(2,1)S(1)}, bf16[128,128]{1,0:T(8,128)(2,1)}, u32[]{:S(2)}) copy-start(bf16[128,128]{1,0:T(8,128)(2,1)} %fw_ref.3) | copy-start | bytes 98308
